TPU v7x, 32 devices: a whole 2x2x4 slice. The times are simulated.
32 devices in a mesh: batch: 2 (over y), space: 16 (over z, x, core).
Axes of the slice: x: 2, y: 2, z: 4, core: 2. Of those that a mesh axis runs over, the one named last changes fastest.
Arguments:
- features: bfloat16 [2, 80, 64, 512], P('batch', 'space'), may hold values from -6 to 6
- cotangent: bfloat16 [2, 80, 64, 512], P('batch', 'space'), may hold values from -6 to 6
- brick_count: int32 [2, 16], P('batch', 'space'), may hold values from 1 to 5, as said below
- destination: int32 [2, 80], P('batch', 'space'), may hold values from -1 to 31, as said below
- neighbours: int32 [2, 26, 80], P('batch', None, 'space'), may hold values from -1 to 4, as said below
- kernel_one: bfloat16 [64, 1728], replicated, may hold values from -0.15625 to 0.15625
- kernel_two: bfloat16 [64, 1728], replicated, may hold values from -0.15625 to 0.15625
Outputs:
- block_output: bfloat16 [2, 32, 64, 512], P('batch', 'space')
- grad_features: bfloat16 [2, 80, 64, 512], P('batch', 'space')
- grad_kernel_one: float32 [64, 1728], replicated
- grad_kernel_two: float32 [64, 1728], replicated
Inputs may be any that keep to these rules, and one draw needn't show every extreme that they name: `brick_count`: A volume holds at most 2 times the devices of space active bricks; some device holds exactly 5. `destination`: -1 exactly on inactive slots. A device's first min(count, 2) bricks go to its own work slots 0, 1, ... in order; its brick in slot 2 + k (k = 0, 1, 2) goes to a work slot of device (s + 1 + k) mod 16; every work slot receives at most one brick, every device receives at most one brick, and a receiving device's own bricks fill its slots below the received one. In every volume some device receives a brick in its work slot 1. `neighbours`: entries of inactive slots are -1; an entry is never the slot of an inactive brick. Bricks sit on a grid of 3 x 3 positions per device, and the offset along the first cell axis is the offset in the device index.
All inputs are finite; a program needn't handle non-finite values.
Results may differ from a plain program's by a relative error of at most 0.0041.
Values may be sent and summed in bfloat16 or wider, within the bound.
No kernel may reach another device: no remote copies, remote signals or barrier semaphores. Data moves between devices by JAX's collectives and lax.ppermute only.
A program may use at most 128 MiB of HBM per device.

v0:
```python
import math

import jax
import jax.numpy as jnp
import numpy as np
from jax import lax
from jax.experimental import pallas as pl
from jax.experimental.pallas import tpu as pltpu
from jax.sharding import PartitionSpec as P

EDGE = 8
WORK_CAP = 2
CELLS = EDGE**3
PLANE = EDGE * EDGE
LONG = CELLS + 2 * PLANE
LANES = 128
SIDES = (-1, 0, 1)
RING = [(q, r) for q in SIDES for r in SIDES]
TURNS = [(q, r) for q, r in RING if (q, r) != (0, 0)]


def turn_tables():
    cell = np.arange(PLANE)
    row, column = cell // EDGE, cell % EDGE
    moves = np.zeros((len(TURNS), 4 * PLANE, 4 * PLANE), np.float32)
    for number, (q, r) in enumerate(TURNS):
        source = ((row + q) % EDGE) * EDGE + (column + r) % EDGE
        for block in range(4):
            moves[number, block * PLANE + source, block * PLANE + cell] = 1
    lane = np.arange(LONG) % PLANE
    edges = np.stack(
        [
            lane // EDGE == EDGE - 1,
            lane // EDGE == 0,
            lane % EDGE == EDGE - 1,
            lane % EDGE == 0,
        ]
    ).astype(np.float32)
    edges = np.broadcast_to(edges[:, None, :], (4, 16, LONG))
    return jnp.asarray(moves, jnp.bfloat16), jnp.asarray(edges, jnp.bfloat16)


def shifted_right(values):
    tail = jnp.zeros((values.shape[0], LONG - CELLS), jnp.float32)
    return pltpu.roll(jnp.concatenate([values, tail], axis=1), PLANE, 1)


def stage(x_ref, dy_ref, long_ref, last_ref, first_ref):
    slots, channels = x_ref.shape[0], x_ref.shape[1]
    for slot in range(slots):
        for half, ref in enumerate((x_ref, dy_ref)):
            long_ref[slot, half * channels : (half + 1) * channels, :] = shifted_right(
                ref[slot].astype(jnp.float32)
            ).astype(jnp.bfloat16)
        last_ref[slot] = long_ref[slot, :, LONG - LANES :]
        first_ref[slot] = long_ref[slot, :, :LANES]
    long_ref[slots] = jnp.zeros(long_ref.shape[1:], jnp.bfloat16)


def gather_sides(slots, low_ref, high_ref, low, high):
    for slot in range(slots):
        low[slot] = low_ref[slot]
        high[slot] = high_ref[slot]
    low[slots] = jnp.zeros(low.shape[1:], jnp.bfloat16)
    high[slots] = jnp.zeros(high.shape[1:], jnp.bfloat16)


def spread(j, slots, link, long_ref, low, high, edge_ref, move_ref, mixed, outs):
    rows = long_ref.shape[1]
    channels = rows // 2
    place = {}
    for p in SIDES:
        for q, r in RING:
            if (p, q, r) == (0, 0, 0):
                place[p, q, r] = j
                continue
            number = 9 * (p + 1) + 3 * (q + 1) + (r + 1)
            number = number if number < 13 else number - 1
            found = link[number * slots + j]
            place[p, q, r] = jnp.where(found < 0, slots, found)
    one = jnp.ones((16, LANES), jnp.bfloat16)
    for tile in range(LONG // LANES):
        span = slice(tile * LANES, (tile + 1) * LANES)
        edge = {
            name: edge_ref[k, :, span]
            for k, name in enumerate((("q", -1), ("q", 1), ("r", -1), ("r", 1)))
        }
        inner = {name: one - value for name, value in edge.items()}
        for part in range(rows // 16):
            band = slice(part * 16, (part + 1) * 16)
            raw = {}
            for q, r in RING:
                value = long_ref[place[0, q, r], band, span]
                if tile == 0:
                    value = value + low[place[-1, q, r], band, :]
                if tile == LONG // LANES - 1:
                    value = value + high[place[1, q, r], band, :]
                raw[q, r] = value
            for r in (-1, 1):
                for q in SIDES:
                    raw[q, r] = raw[q, 0] * inner["r", r] + raw[q, r] * edge["r", r]
            for number, (q, r) in enumerate(TURNS):
                value = raw[q, r]
                if q != 0:
                    value = raw[0, r] * inner["q", q] + raw[q, r] * edge["q", q]
                mixed[number, band, span] = value
            half, start = divmod(part * 16, channels)
            start += 4 * channels
            outs[half][start : start + 16, span] = raw[0, 0]
    for number, (q, r) in enumerate(TURNS):
        start = RING.index((q, r)) * channels
        for low_lane in range(0, LONG, 4 * PLANE):
            width = min(4 * PLANE, LONG - low_lane)
            moved = jnp.dot(
                mixed[number, :, low_lane : low_lane + width],
                move_ref[number, :width, :width],
                preferred_element_type=jnp.float32,
            ).astype(jnp.bfloat16)
            for half in range(2):
                outs[half][start : start + channels, low_lane : low_lane + width] = moved[
                    half * channels : (half + 1) * channels
                ]


def convolved(weight_ref, field):
    channels = weight_ref.shape[0] // 3
    parts = jnp.dot(weight_ref[...], field[...], preferred_element_type=jnp.float32)
    middle = pltpu.roll(parts[channels : 2 * channels], LONG - PLANE, 1)
    return (
        parts[:channels, :CELLS] + middle[:, :CELLS] + parts[2 * channels :, LONG - CELLS :]
    )


def three_ways(values, moved):
    tail = jnp.zeros((values.shape[0], LONG - CELLS), jnp.float32)
    return jnp.concatenate(
        [
            jnp.concatenate([values, tail], axis=1).astype(jnp.bfloat16),
            moved,
            jnp.concatenate([tail, values], axis=1).astype(jnp.bfloat16),
        ],
        axis=0,
    )


def first_half(
    link, count, long_ref, low_ref, high_ref, edge_ref, move_ref, one_ref, two_ref,
    inner_ref, last_ref, first_ref, grad_ref,
    low, high, mixed, field_x, field_dy, sum_one, sum_two,
):
    slots = low_ref.shape[0]
    channels = long_ref.shape[1] // 2
    gather_sides(slots, low_ref, high_ref, low, high)
    sum_one[...] = jnp.zeros_like(sum_one)
    sum_two[...] = jnp.zeros_like(sum_two)
    inner_ref[...] = jnp.zeros_like(inner_ref)

    def visit(j, carry):
        spread(
            j, slots, link, long_ref, low, high, edge_ref, move_ref, mixed, (field_x, field_dy)
        )
        pre = convolved(one_ref, field_x)
        grad_hidden = convolved(two_ref, field_dy)
        sigma = 1.0 / (1.0 + jnp.exp(-pre))
        hidden = pre * sigma
        grad_pre = grad_hidden * (sigma * (1.0 + pre * (1.0 - sigma)))
        hidden_long = shifted_right(hidden).astype(jnp.bfloat16)
        grad_long = shifted_right(grad_pre).astype(jnp.bfloat16)
        inner_ref[j, :channels, :] = hidden_long
        inner_ref[j, channels:, :] = grad_long
        sum_one[...] += lax.dot_general(
            three_ways(grad_pre, grad_long),
            field_x[...],
            (((1,), (1,)), ((), ())),
            preferred_element_type=jnp.float32,
        )
        sum_two[...] += lax.dot_general(
            field_dy[...],
            three_ways(hidden, hidden_long),
            (((1,), (1,)), ((), ())),
            preferred_element_type=jnp.float32,
        )
        return carry

    lax.fori_loop(0, count[0], visit, 0)
    for slot in range(slots):
        last_ref[slot] = inner_ref[slot, :, LONG - LANES :]
        first_ref[slot] = inner_ref[slot, :, :LANES]
    grad_ref[:channels, :] = jnp.concatenate(
        [sum_one[p * channels : (p + 1) * channels, :] for p in range(3)], axis=1
    )
    blocks = []
    for tap in range(27):
        p, rest = divmod(26 - tap, 9)
        blocks.append(
            sum_two[rest * channels : (rest + 1) * channels, p * channels : (p + 1) * channels]
        )
    grad_ref[channels:, :] = jnp.concatenate(blocks, axis=1)


def second_half(
    link, count, inner_ref, low_ref, high_ref, edge_ref, move_ref, two_ref, one_ref, x_ref, dy_ref,
    out_ref, back_ref,
    low, high, mixed, field_h, field_g,
):
    slots = low_ref.shape[0]
    gather_sides(slots, low_ref, high_ref, low, high)
    out_ref[...] = jnp.zeros_like(out_ref)
    back_ref[...] = jnp.zeros_like(back_ref)

    def visit(j, carry):
        spread(
            j, slots, link, inner_ref, low, high, edge_ref, move_ref, mixed, (field_h, field_g)
        )
        out = convolved(two_ref, field_h)
        back = convolved(one_ref, field_g).astype(jnp.bfloat16)
        out_ref[j] = (x_ref[j].astype(jnp.float32) + out).astype(jnp.bfloat16)
        back_ref[j] = (dy_ref[j].astype(jnp.float32) + back.astype(jnp.float32)).astype(
            jnp.bfloat16
        )
        return carry

    lax.fori_loop(0, count[0], visit, 0)


def vmem(count):
    return [pl.BlockSpec(memory_space=pltpu.VMEM)] * count


def smem(count):
    return [pl.BlockSpec(memory_space=pltpu.SMEM)] * count


def step_to(x, by, wrap):
    size = lax.axis_size("space")
    pairs = [(i, (i + by) % size) for i in range(size) if wrap or 0 <= i + by < size]
    return lax.ppermute(x, "space", pairs)


def all_sum(rows):
    levels = []
    for axis in ("space", "batch"):
        reach = 1
        while reach < lax.axis_size(axis):
            levels.append((axis, reach))
            reach *= 2

    def swap(value, axis, reach):
        size = lax.axis_size(axis)
        return lax.ppermute(value, axis, [(i, i ^ reach) for i in range(size)])

    taken = []
    for number, (axis, reach) in enumerate(levels):
        wire = jnp.float32 if number == 0 or rows.shape[0] <= 16 else jnp.bfloat16
        if rows.shape[0] > 8:
            upper = (lax.axis_index(axis) // reach) % 2 == 1
            middle = rows.shape[0] // 2
            keep = jnp.where(upper, rows[middle:], rows[:middle])
            give = jnp.where(upper, rows[:middle], rows[middle:]).astype(wire)
            rows = keep + swap(give, axis, reach).astype(jnp.float32)
            taken.append((axis, reach, upper))
        else:
            rows = rows + swap(rows, axis, reach)
    rows = rows.astype(jnp.bfloat16)
    for axis, reach, upper in taken[::-1]:
        other = swap(rows, axis, reach)
        rows = jnp.concatenate(
            [jnp.where(upper, other, rows), jnp.where(upper, rows, other)], axis=0
        )
    return rows


def shards(features, cotangent, brick_count, destination, neighbours, kernel_one, kernel_two):
    slots, channels = features.shape[1], features.shape[2]
    taps = kernel_one.shape[1] // channels
    x, dy = features[0], cotangent[0]
    count = brick_count[0]
    link = neighbours[0].reshape(-1)
    bf16, f32 = jnp.bfloat16, jnp.float32
    shape = jax.ShapeDtypeStruct
    long_shape = shape((slots + 1, 2 * channels, LONG), bf16)
    side_shape = shape((slots, 2 * channels, LANES), bf16)
    moves, edges = turn_tables()

    def straight(kernel):
        return (
            kernel.reshape(channels, 3, 9 * channels)
            .transpose(1, 0, 2)
            .reshape(3 * channels, 9 * channels)
        )

    def turned(kernel):
        return (
            kernel.reshape(channels, taps, channels)[:, ::-1]
            .reshape(channels, 3, 9, channels)
            .transpose(1, 3, 2, 0)
            .reshape(3 * channels, 9 * channels)
        )

    long_in, last, first = pl.pallas_call(
        stage,
        out_shape=(long_shape, side_shape, side_shape),
        in_specs=vmem(2),
        out_specs=tuple(vmem(3)),
        name="stage",
    )(x, dy)
    low = step_to(last, 1, False)
    high = step_to(first, -1, False)
    side_scratch = pltpu.VMEM((slots + 1, 2 * channels, LANES), bf16)
    mixed_scratch = pltpu.VMEM((len(TURNS), 2 * channels, LONG), bf16)
    field_scratch = pltpu.VMEM((9 * channels, LONG), bf16)
    inner, inner_last, inner_first, grads = pl.pallas_call(
        first_half,
        out_shape=(
            long_shape,
            side_shape,
            side_shape,
            shape((2 * channels, taps * channels), f32),
        ),
        in_specs=smem(2) + vmem(7),
        out_specs=tuple(vmem(4)),
        scratch_shapes=[
            side_scratch,
            side_scratch,
            mixed_scratch,
            field_scratch,
            field_scratch,
            pltpu.VMEM((3 * channels, 9 * channels), f32),
            pltpu.VMEM((9 * channels, 3 * channels), f32),
        ],
        name="first_half",
    )(link, count, long_in, low, high, edges, moves, straight(kernel_one), turned(kernel_two))
    inner_low = step_to(inner_last, 1, False)
    inner_high = step_to(inner_first, -1, False)
    out, grad_in = pl.pallas_call(
        second_half,
        out_shape=(shape(x.shape, bf16), shape(x.shape, bf16)),
        in_specs=smem(2) + vmem(9),
        out_specs=tuple(vmem(2)),
        scratch_shapes=[side_scratch, side_scratch, mixed_scratch, field_scratch, field_scratch],
        name="second_half",
    )(
        link, count, inner, inner_low, inner_high, edges, moves,
        straight(kernel_two), turned(kernel_one), x, dy,
    )
    arrived = jnp.zeros_like(out[0])
    for step in range(slots - WORK_CAP):
        arrived = arrived + step_to(out[WORK_CAP + step], step + 1, True)
    free = (jnp.arange(WORK_CAP, dtype=jnp.int32) == count[0])[:, None, None]
    placed = jnp.where(free, arrived[None], out[:WORK_CAP])
    scale = 1.0 / math.sqrt(
        lax.axis_size("batch") * features.shape[0] * lax.axis_size("space") * slots * CELLS
    )
    total = all_sum(grads).astype(f32) * scale
    return (placed[None], grad_in[None], total[:channels], total[channels:])


def solution(mesh):
    return jax.shard_map(
        shards,
        mesh=mesh,
        in_specs=(
            P("batch", "space", None, None),
            P("batch", "space", None, None),
            P("batch", "space"),
            P("batch", "space"),
            P("batch", None, "space"),
            P(),
            P(),
        ),
        out_specs=(P("batch", "space", None, None), P("batch", "space", None, None), P(), P()),
        check_vma=False,
    )
```

profile of v0, /device:TPU:1, one launch (start us, length us, event | category | flops | bytes accessed | tf_op | source)
XLA Modules:
  0.0 88.9 jit_solution(2136155171291570177)
XLA Ops:
  0.6 2.4 %stage.1 = (bf16[6,128,640]{2,1,0:T(8,128)(2,1)}, bf16[5,128,128]{2,1,0:T(8,128)(2,1)}, bf16[5,128,128]{2,1,0:T(8,128)(2,1)}) custom-call(bf16[5,64,512]{2,1,0:T(8,128)(2,1)} %bitcast.30, bf16[5,64,512]{2,1,0:T(8,128)(2,1)} %bitcast.32), custom_call_target="tpu_custom_call" | custom-call | tf_op jit(solution)/shard_map/stage/pallas_call | solution.py:300
  3.1 4.5 %collective-permute-start = (bf16[5,128,128]{2,1,0:T(8,128)(2,1)}, bf16[5,128,128]{2,1,0:T(8,128)(2,1)S(1)}, u32[]{:S(2)}, u32[]{:S(2)}) collective-permute-start(bf16[5,128,128]{2,1,0:T(8,128)(2,1)} %get-tuple-element.14), channel_id=1, source_target_pairs={{0,1},{1,2},{2,3},{3,4},{4,5},{5,6},{6,7},{7,8},{8,9},{9,10},{10,1... | collective-permute-start | bytes 491528 | tf_op jit(solution)/shard_map/ppermute | solution.py:237
  7.6 1.9 %collective-permute-start.1 = (bf16[5,128,128]{2,1,0:T(8,128)(2,1)}, bf16[5,128,128]{2,1,0:T(8,128)(2,1)S(1)}, u32[]{:S(2)}, u32[]{:S(2)}) collective-permute-start(bf16[5,128,128]{2,1,0:T(8,128)(2,1)} %get-tuple-element.15), channel_id=1, source_target_pairs={{1,0},{2,1},{3,2},{4,3},{5,4},{6,5},{7,6},{8,7},{9,8},{10,9},{11,1... | collective-permute-start | bytes 491528 | tf_op jit(solution)/shard_map/ppermute | solution.py:237
  9.5 0.7 copy-done.7
  10.2 0.1 copy.14
  10.3 0.7 reshape_squeeze.3.link
  11.6 0.2 reshape.43
  11.8 0.7 copy.15
  12.5 0.3 copy-done.1
  12.8 0.5 reshape.45
  13.3 0.5 rev.6
  13.9 0.2 copy.16
  14.1 0.6 copy.23
  14.7 1.1 %reshape.53.two_ref = bf16[192,576]{1,0:T(8,128)(2,1)} reshape(bf16[3,64,9,64]{3,2,1,0:T(8,128)(2,1)S(1)} %copy.23) | data formatting | bytes 442368 | tf_op jit(solution)/shard_map/reshape | solution.py:297
  15.8 0.6 copy-done.3
  16.5 5.4 %first_half.1 = (bf16[6,128,640]{2,1,0:T(8,128)(2,1)}, bf16[5,128,128]{2,1,0:T(8,128)(2,1)}, bf16[5,128,128]{2,1,0:T(8,128)(2,1)}, f32[128,1728]{1,0:T(8,128)}) custom-call(s32[130]{0:T(256)} %reshape_squeeze.3.link, s32[1]{0:T(128)} %bitcast.24.count, bf16[6,128,640]{2,1,0:T(8,128)(2,1)} %get-tuple-element.13.long_ref, bf16[5,128,128]{2,1,0:T(8,128)(2,1)} %copy-done.3, ...), custom_call_target="tpu_custom_call" | custom-call | tf_op jit(solution)/shard_map/first_half/pallas_call | solution.py:312
  21.9 1.3 %slice_select_fusion = f32[64,1728]{1,0:T(8,128)S(1)} fusion(f32[128,1728]{1,0:T(8,128)} %get-tuple-element.21, pred[]{:T(512)S(6)} %eq.29), kind=kLoop, calls=%fused_computation.2 | loop fusion | flops 110592 | bytes 1327105 | tf_op jit(solution)/shard_map/jit(_where)/select_n | solution.py:259
  23.2 5.6 %collective-permute-start.7 = (f32[64,1728]{1,0:T(8,128)S(1)}, f32[64,1728]{1,0:T(8,128)S(1)}, u32[]{:S(2)}, u32[]{:S(2)}) collective-permute-start(f32[64,1728]{1,0:T(8,128)S(1)} %slice_select_fusion), channel_id=1, source_target_pairs={{0,1},{1,0},{2,3},{3,2},{4,5},{5,4},{6,7},{7,6},{8,9},{9,8},{10,11... | collective-permute-start | bytes 1327112 | tf_op jit(solution)/shard_map/ppermute | solution.py:250
  28.8 1.4 %collective-permute-done.7 = f32[64,1728]{1,0:T(8,128)S(1)} collective-permute-done((f32[64,1728]{1,0:T(8,128)S(1)}, f32[64,1728]{1,0:T(8,128)S(1)}, u32[]{:S(2)}, u32[]{:S(2)}) %collective-permute-start.7) | collective-permute-done | bytes 442400 | tf_op jit(solution)/shard_map/ppermute | solution.py:250
  30.4 0.1 collective-permute-start.8
  30.5 4.3 %collective-permute-done.8 = bf16[32,1728]{1,0:T(8,128)(2,1)S(1)} collective-permute-done((bf16[32,1728]{1,0:T(8,128)(2,1)S(1)}, bf16[32,1728]{1,0:T(8,128)(2,1)S(1)}, u32[]{:S(2)}, u32[]{:S(2)}) %collective-permute-start.8) | collective-permute-done | bytes 110624 | tf_op jit(solution)/shard_map/ppermute | solution.py:250
  34.8 3.5 %collective-permute-start.9 = (bf16[16,1728]{1,0:T(8,128)(2,1)S(1)}, bf16[16,1728]{1,0:T(8,128)(2,1)S(1)}, u32[]{:S(2)}, u32[]{:S(2)}) collective-permute-start(bf16[16,1728]{1,0:T(8,128)(2,1)S(1)} %select_convert_fusion.1), channel_id=1, source_target_pairs={{0,4},{1,5},{2,6},{3,7},{4,0},{5,1},{6,2},{7,3},{8,12},{9,13},{10,... | collective-permute-start | bytes 165896 | tf_op jit(solution)/shard_map/ppermute | solution.py:250
  38.4 1.6 %collective-permute-done.9 = bf16[16,1728]{1,0:T(8,128)(2,1)S(1)} collective-permute-done((bf16[16,1728]{1,0:T(8,128)(2,1)S(1)}, bf16[16,1728]{1,0:T(8,128)(2,1)S(1)}, u32[]{:S(2)}, u32[]{:S(2)}) %collective-permute-start.9) | collective-permute-done | bytes 55328 | tf_op jit(solution)/shard_map/ppermute | solution.py:250
  40.0 4.6 %collective-permute-start.10 = (f32[8,1728]{1,0:T(8,128)S(1)}, f32[8,1728]{1,0:T(8,128)S(1)}, u32[]{:S(2)}, u32[]{:S(2)}) collective-permute-start(f32[8,1728]{1,0:T(8,128)S(1)} %slice_select_fusion.1), channel_id=1, source_target_pairs={{0,8},{1,9},{2,10},{3,11},{4,12},{5,13},{6,14},{7,15},{8,0},{9,1},... | collective-permute-start | bytes 165896 | tf_op jit(solution)/shard_map/ppermute | solution.py:250
  44.6 2.0 %collective-permute-done.10 = f32[8,1728]{1,0:T(8,128)S(1)} collective-permute-done((f32[8,1728]{1,0:T(8,128)S(1)}, f32[8,1728]{1,0:T(8,128)S(1)}, u32[]{:S(2)}, u32[]{:S(2)}) %collective-permute-start.10) | collective-permute-done | bytes 55328 | tf_op jit(solution)/shard_map/ppermute | solution.py:250
  46.7 6.4 %collective-permute-start.2 = (bf16[5,128,128]{2,1,0:T(8,128)(2,1)S(1)}, bf16[5,128,128]{2,1,0:T(8,128)(2,1)S(1)}, u32[]{:S(2)}, u32[]{:S(2)}) collective-permute-start(bf16[5,128,128]{2,1,0:T(8,128)(2,1)S(1)} %copy-done.9), channel_id=1, source_target_pairs={{0,1},{1,2},{2,3},{3,4},{4,5},{5,6},{6,7},{7,8},{8,9},{9,10},{10,1... | collective-permute-start | bytes 491528 | tf_op jit(solution)/shard_map/ppermute | solution.py:237
  53.1 1.9 %collective-permute-start.3 = (bf16[5,128,128]{2,1,0:T(8,128)(2,1)S(1)}, bf16[5,128,128]{2,1,0:T(8,128)(2,1)S(1)}, u32[]{:S(2)}, u32[]{:S(2)}) collective-permute-start(bf16[5,128,128]{2,1,0:T(8,128)(2,1)S(1)} %copy-done.8), channel_id=1, source_target_pairs={{1,0},{2,1},{3,2},{4,3},{5,4},{6,5},{7,6},{8,7},{9,8},{10,9},{11,1... | collective-permute-start | bytes 491528 | tf_op jit(solution)/shard_map/ppermute | solution.py:237
  55.1 2.8 %collective-permute-start.12 = (bf16[8,1728]{1,0:T(8,128)(2,1)S(1)}, bf16[8,1728]{1,0:T(8,128)(2,1)S(1)}, u32[]{:S(2)}, u32[]{:S(2)}) collective-permute-start(bf16[8,1728]{1,0:T(8,128)(2,1)S(1)} %add_convert_fusion), channel_id=1, source_target_pairs={{0,8},{1,9},{2,10},{3,11},{4,12},{5,13},{6,14},{7,15},{8,0},{9,1},... | collective-permute-start | bytes 82952 | tf_op jit(solution)/shard_map/ppermute | solution.py:250
  57.8 0.2 reshape.48
  58.0 0.5 reshape.50
  58.5 0.7 copy.19
  59.2 0.5 rev.7
  59.8 0.2 copy.20
  59.9 0.6 copy.24
  60.6 1.1 %reshape.54.one_ref = bf16[192,576]{1,0:T(8,128)(2,1)} reshape(bf16[3,64,9,64]{3,2,1,0:T(8,128)(2,1)S(1)} %copy.24) | data formatting | bytes 442368 | tf_op jit(solution)/shard_map/reshape | solution.py:297
  61.7 0.6 copy-done.5
  62.4 4.4 %second_half.1 = (bf16[5,64,512]{2,1,0:T(8,128)(2,1)}, bf16[5,64,512]{2,1,0:T(8,128)(2,1)}) custom-call(s32[130]{0:T(256)} %reshape_squeeze.3.link, s32[1]{0:T(128)} %bitcast.25.count, bf16[6,128,640]{2,1,0:T(8,128)(2,1)} %get-tuple-element.16.inner_ref, bf16[5,128,128]{2,1,0:T(8,128)(2,1)} %copy-done.5, bf16[5,128,128]{2,1,0:T(8,128)(2,1)} %copy-done.6, ...), custom_call_target="tpu_custom_call" | custom-call | tf_op jit(solution)/shard_map/second_half/pallas_call | solution.py:335
  66.8 1.8 %collective-permute-start.13 = (bf16[16,1728]{1,0:T(8,128)(2,1)S(1)}, bf16[16,1728]{1,0:T(8,128)(2,1)S(1)}, u32[]{:S(2)}, u32[]{:S(2)}) collective-permute-start(bf16[16,1728]{1,0:T(8,128)(2,1)S(1)} %pad_maximum_fusion.2), channel_id=1, source_target_pairs={{0,4},{1,5},{2,6},{3,7},{4,0},{5,1},{6,2},{7,3},{8,12},{9,13},{10,... | collective-permute-start | bytes 165896 | tf_op jit(solution)/shard_map/ppermute | solution.py:250
  68.6 0.9 %slice_bitcast_fusion.1 = (bf16[64,512]{1,0:T(8,128)(2,1)S(1)}, bf16[64,512]{1,0:T(8,128)(2,1)S(1)}, bf16[64,512]{1,0:T(8,128)(2,1)S(1)}) fusion(bf16[5,64,512]{2,1,0:T(8,128)(2,1)} %get-tuple-element.19), kind=kLoop, calls=%fused_computation.16 | loop fusion | bytes 393216 | tf_op jit(solution)/shard_map/squeeze | solution.py:348
  69.5 7.4 %collective-permute-start.6 = (bf16[64,512]{1,0:T(8,128)(2,1)S(1)}, bf16[64,512]{1,0:T(8,128)(2,1)S(1)}, u32[]{:S(2)}, u32[]{:S(2)}) collective-permute-start(bf16[64,512]{1,0:T(8,128)(2,1)S(1)} %get-tuple-element.27), channel_id=1, source_target_pairs={{0,3},{1,4},{2,5},{3,6},{4,7},{5,8},{6,9},{7,10},{8,11},{9,12},{10... | collective-permute-start | bytes 196616 | tf_op jit(solution)/shard_map/ppermute | solution.py:237
  76.9 1.2 %collective-permute-start.5 = (bf16[64,512]{1,0:T(8,128)(2,1)S(1)}, bf16[64,512]{1,0:T(8,128)(2,1)S(1)}, u32[]{:S(2)}, u32[]{:S(2)}) collective-permute-start(bf16[64,512]{1,0:T(8,128)(2,1)S(1)} %get-tuple-element.26), channel_id=1, source_target_pairs={{0,2},{1,3},{2,4},{3,5},{4,6},{5,7},{6,8},{7,9},{8,10},{9,11},{10,... | collective-permute-start | bytes 196616 | tf_op jit(solution)/shard_map/ppermute | solution.py:237
  78.3 4.5 %collective-permute-done.5 = bf16[64,512]{1,0:T(8,128)(2,1)S(1)} collective-permute-done((bf16[64,512]{1,0:T(8,128)(2,1)S(1)}, bf16[64,512]{1,0:T(8,128)(2,1)S(1)}, u32[]{:S(2)}, u32[]{:S(2)}) %collective-permute-start.5) | collective-permute-done | bytes 65568 | tf_op jit(solution)/shard_map/ppermute | solution.py:237
  82.8 2.5 %collective-permute-done.14 = bf16[32,1728]{1,0:T(8,128)(2,1)S(1)} collective-permute-done((bf16[32,1728]{1,0:T(8,128)(2,1)S(1)}, bf16[32,1728]{1,0:T(8,128)(2,1)S(1)}, u32[]{:S(2)}, u32[]{:S(2)}) %collective-permute-start.14) | collective-permute-done | bytes 110624 | tf_op jit(solution)/shard_map/ppermute | solution.py:250
  85.5 0.6 collective-permute-start.15
  86.1 1.6 %select_bitcast_fusion = bf16[1,2,64,512]{3,2,1,0:T(8,128)(2,1)} fusion(bf16[5,64,512]{2,1,0:T(8,128)(2,1)} %get-tuple-element.19, pred[2]{0:T(512)(128)(4,1)S(1)} %iota_compare_fusion, bf16[64,512]{1,0:T(8,128)(2,1)S(1)} %add_add_fusion), kind=kLoop, calls=%fused_computation.8 | loop fusion | flops 65536 | bytes 327682 | tf_op jit(solution)/shard_map/broadcast_in_dim | solution.py:355
  87.7 0.1 broadcast_select_fusion.1
  87.8 0.1 convert_multiply_fusion
  87.9 1.0 %fusion = (f32[64,1728]{1,0:T(8,128)}, f32[64,1728]{1,0:T(8,128)}) fusion(f32[128,1728]{1,0:T(8,128)S(1)} %convert_multiply_fusion), kind=kLoop, calls=%fused_computation.27 | loop fusion | bytes 1769472 | tf_op jit(solution)/shard_map/slice | solution.py:355
  (45 shorter events, 0.7 us)
Async XLA Ops:
  0.6 11.0 %copy-start.2 = (bf16[64,1728]{1,0:T(8,128)(2,1)S(1)}, bf16[64,1728]{1,0:T(8,128)(2,1)}, u32[]{:S(2)}) copy-start(bf16[64,1728]{1,0:T(8,128)(2,1)} %param.13) | copy-start | bytes 663556
  3.1 12.7 %collective-permute-start = (bf16[5,128,128]{2,1,0:T(8,128)(2,1)}, bf16[5,128,128]{2,1,0:T(8,128)(2,1)S(1)}, u32[]{:S(2)}, u32[]{:S(2)}) collective-permute-start(bf16[5,128,128]{2,1,0:T(8,128)(2,1)} %get-tuple-element.14), channel_id=1, source_target_pairs={{0,1},{1,2},{2,3},{3,4},{4,5},{5,6},{6,7},{7,8},{8,9},{9,10},{10,1... | collective-permute-start | bytes 491528 | tf_op jit(solution)/shard_map/ppermute | solution.py:237
  7.6 8.2 %collective-permute-start.1 = (bf16[5,128,128]{2,1,0:T(8,128)(2,1)}, bf16[5,128,128]{2,1,0:T(8,128)(2,1)S(1)}, u32[]{:S(2)}, u32[]{:S(2)}) collective-permute-start(bf16[5,128,128]{2,1,0:T(8,128)(2,1)} %get-tuple-element.15), channel_id=1, source_target_pairs={{1,0},{2,1},{3,2},{4,3},{5,4},{6,5},{7,6},{8,7},{9,8},{10,9},{11,1... | collective-permute-start | bytes 491528 | tf_op jit(solution)/shard_map/ppermute | solution.py:237
  9.5 0.7 copy-start.7
  11.8 1.0 %copy-start.1 = (bf16[64,1728]{1,0:T(8,128)(2,1)S(1)}, bf16[64,1728]{1,0:T(8,128)(2,1)}, u32[]{:S(2)}) copy-start(bf16[64,1728]{1,0:T(8,128)(2,1)} %param.14) | copy-start | bytes 663556
  15.8 0.7 copy-start.3
  15.8 0.7 copy-start.4
  21.9 8.3 %copy-start = (f32[128,1728]{1,0:T(8,128)S(1)}, f32[128,1728]{1,0:T(8,128)}, u32[]{:S(2)}) copy-start(f32[128,1728]{1,0:T(8,128)} %get-tuple-element.21) | copy-start | bytes 2654212
  23.2 7.0 %collective-permute-start.7 = (f32[64,1728]{1,0:T(8,128)S(1)}, f32[64,1728]{1,0:T(8,128)S(1)}, u32[]{:S(2)}, u32[]{:S(2)}) collective-permute-start(f32[64,1728]{1,0:T(8,128)S(1)} %slice_select_fusion), channel_id=1, source_target_pairs={{0,1},{1,0},{2,3},{3,2},{4,5},{5,4},{6,7},{7,6},{8,9},{9,8},{10,11... | collective-permute-start | bytes 1327112 | tf_op jit(solution)/shard_map/ppermute | solution.py:250
  30.4 4.4 %collective-permute-start.8 = (bf16[32,1728]{1,0:T(8,128)(2,1)S(1)}, bf16[32,1728]{1,0:T(8,128)(2,1)S(1)}, u32[]{:S(2)}, u32[]{:S(2)}) collective-permute-start(bf16[32,1728]{1,0:T(8,128)(2,1)S(1)} %select_convert_fusion), channel_id=1, source_target_pairs={{0,2},{1,3},{2,0},{3,1},{4,6},{5,7},{6,4},{7,5},{8,10},{9,11},{10,... | collective-permute-start | bytes 331784 | tf_op jit(solution)/shard_map/ppermute | solution.py:250
  34.8 5.1 %collective-permute-start.9 = (bf16[16,1728]{1,0:T(8,128)(2,1)S(1)}, bf16[16,1728]{1,0:T(8,128)(2,1)S(1)}, u32[]{:S(2)}, u32[]{:S(2)}) collective-permute-start(bf16[16,1728]{1,0:T(8,128)(2,1)S(1)} %select_convert_fusion.1), channel_id=1, source_target_pairs={{0,4},{1,5},{2,6},{3,7},{4,0},{5,1},{6,2},{7,3},{8,12},{9,13},{10,... | collective-permute-start | bytes 165896 | tf_op jit(solution)/shard_map/ppermute | solution.py:250
  40.0 6.8 %copy-start.9 = (bf16[5,128,128]{2,1,0:T(8,128)(2,1)S(1)}, bf16[5,128,128]{2,1,0:T(8,128)(2,1)}, u32[]{:S(2)}) copy-start(bf16[5,128,128]{2,1,0:T(8,128)(2,1)} %get-tuple-element.17) | copy-start | bytes 491524
  40.0 13.1 %copy-start.8 = (bf16[5,128,128]{2,1,0:T(8,128)(2,1)S(1)}, bf16[5,128,128]{2,1,0:T(8,128)(2,1)}, u32[]{:S(2)}) copy-start(bf16[5,128,128]{2,1,0:T(8,128)(2,1)} %get-tuple-element.18) | copy-start | bytes 491524
  40.0 6.6 %collective-permute-start.10 = (f32[8,1728]{1,0:T(8,128)S(1)}, f32[8,1728]{1,0:T(8,128)S(1)}, u32[]{:S(2)}, u32[]{:S(2)}) collective-permute-start(f32[8,1728]{1,0:T(8,128)S(1)} %slice_select_fusion.1), channel_id=1, source_target_pairs={{0,8},{1,9},{2,10},{3,11},{4,12},{5,13},{6,14},{7,15},{8,0},{9,1},... | collective-permute-start | bytes 165896 | tf_op jit(solution)/shard_map/ppermute | solution.py:250
  46.6 8.4 %collective-permute-start.11 = (f32[8,1728]{1,0:T(8,128)S(1)}, f32[8,1728]{1,0:T(8,128)S(1)}, u32[]{:S(2)}, u32[]{:S(2)}) collective-permute-start(f32[8,1728]{1,0:T(8,128)S(1)} %select_add_fusion.1), channel_id=1, source_target_pairs={{0,16},{16,0},{1,17},{17,1},{2,18},{18,2},{3,19},{19,3},{4,20},{20... | collective-permute-start | bytes 165896 | tf_op jit(solution)/shard_map/ppermute | solution.py:250
  46.7 14.9 %collective-permute-start.2 = (bf16[5,128,128]{2,1,0:T(8,128)(2,1)S(1)}, bf16[5,128,128]{2,1,0:T(8,128)(2,1)S(1)}, u32[]{:S(2)}, u32[]{:S(2)}) collective-permute-start(bf16[5,128,128]{2,1,0:T(8,128)(2,1)S(1)} %copy-done.9), channel_id=1, source_target_pairs={{0,1},{1,2},{2,3},{3,4},{4,5},{5,6},{6,7},{7,8},{8,9},{9,10},{10,1... | collective-permute-start | bytes 491528 | tf_op jit(solution)/shard_map/ppermute | solution.py:237
  53.1 8.5 %collective-permute-start.3 = (bf16[5,128,128]{2,1,0:T(8,128)(2,1)S(1)}, bf16[5,128,128]{2,1,0:T(8,128)(2,1)S(1)}, u32[]{:S(2)}, u32[]{:S(2)}) collective-permute-start(bf16[5,128,128]{2,1,0:T(8,128)(2,1)S(1)} %copy-done.8), channel_id=1, source_target_pairs={{1,0},{2,1},{3,2},{4,3},{5,4},{6,5},{7,6},{8,7},{9,8},{10,9},{11,1... | collective-permute-start | bytes 491528 | tf_op jit(solution)/shard_map/ppermute | solution.py:237
  55.1 11.7 %collective-permute-start.12 = (bf16[8,1728]{1,0:T(8,128)(2,1)S(1)}, bf16[8,1728]{1,0:T(8,128)(2,1)S(1)}, u32[]{:S(2)}, u32[]{:S(2)}) collective-permute-start(bf16[8,1728]{1,0:T(8,128)(2,1)S(1)} %add_convert_fusion), channel_id=1, source_target_pairs={{0,8},{1,9},{2,10},{3,11},{4,12},{5,13},{6,14},{7,15},{8,0},{9,1},... | collective-permute-start | bytes 82952 | tf_op jit(solution)/shard_map/ppermute | solution.py:250
  61.7 0.7 copy-start.5
  61.7 0.7 copy-start.6
  66.8 11.4 %collective-permute-start.13 = (bf16[16,1728]{1,0:T(8,128)(2,1)S(1)}, bf16[16,1728]{1,0:T(8,128)(2,1)S(1)}, u32[]{:S(2)}, u32[]{:S(2)}) collective-permute-start(bf16[16,1728]{1,0:T(8,128)(2,1)S(1)} %pad_maximum_fusion.2), channel_id=1, source_target_pairs={{0,4},{1,5},{2,6},{3,7},{4,0},{5,1},{6,2},{7,3},{8,12},{9,13},{10,... | collective-permute-start | bytes 165896 | tf_op jit(solution)/shard_map/ppermute | solution.py:250
  69.5 8.8 %collective-permute-start.6 = (bf16[64,512]{1,0:T(8,128)(2,1)S(1)}, bf16[64,512]{1,0:T(8,128)(2,1)S(1)}, u32[]{:S(2)}, u32[]{:S(2)}) collective-permute-start(bf16[64,512]{1,0:T(8,128)(2,1)S(1)} %get-tuple-element.27), channel_id=1, source_target_pairs={{0,3},{1,4},{2,5},{3,6},{4,7},{5,8},{6,9},{7,10},{8,11},{9,12},{10... | collective-permute-start | bytes 196616 | tf_op jit(solution)/shard_map/ppermute | solution.py:237
  76.9 1.4 %collective-permute-start.4 = (bf16[64,512]{1,0:T(8,128)(2,1)S(1)}, bf16[64,512]{1,0:T(8,128)(2,1)S(1)}, u32[]{:S(2)}, u32[]{:S(2)}) collective-permute-start(bf16[64,512]{1,0:T(8,128)(2,1)S(1)} %get-tuple-element.28), channel_id=1, source_target_pairs={{0,1},{1,2},{2,3},{3,4},{4,5},{5,6},{6,7},{7,8},{8,9},{9,10},{10,1... | collective-permute-start | bytes 196616 | tf_op jit(solution)/shard_map/ppermute | solution.py:237
  76.9 5.9 %collective-permute-start.5 = (bf16[64,512]{1,0:T(8,128)(2,1)S(1)}, bf16[64,512]{1,0:T(8,128)(2,1)S(1)}, u32[]{:S(2)}, u32[]{:S(2)}) collective-permute-start(bf16[64,512]{1,0:T(8,128)(2,1)S(1)} %get-tuple-element.26), channel_id=1, source_target_pairs={{0,2},{1,3},{2,4},{3,5},{4,6},{5,7},{6,8},{7,9},{8,10},{9,11},{10,... | collective-permute-start | bytes 196616 | tf_op jit(solution)/shard_map/ppermute | solution.py:237
  78.2 7.2 %collective-permute-start.14 = (bf16[32,1728]{1,0:T(8,128)(2,1)S(1)}, bf16[32,1728]{1,0:T(8,128)(2,1)S(1)}, u32[]{:S(2)}, u32[]{:S(2)}) collective-permute-start(bf16[32,1728]{1,0:T(8,128)(2,1)S(1)} %pad_maximum_fusion.1), channel_id=1, source_target_pairs={{0,2},{1,3},{2,0},{3,1},{4,6},{5,7},{6,4},{7,5},{8,10},{9,11},{10,... | collective-permute-start | bytes 331784 | tf_op jit(solution)/shard_map/ppermute | solution.py:250
  85.5 2.3 %collective-permute-start.15 = (bf16[64,1728]{1,0:T(8,128)(2,1)S(1)}, bf16[64,1728]{1,0:T(8,128)(2,1)S(1)}, u32[]{:S(2)}, u32[]{:S(2)}) collective-permute-start(bf16[64,1728]{1,0:T(8,128)(2,1)S(1)} %pad_maximum_fusion), channel_id=1, source_target_pairs={{0,1},{1,0},{2,3},{3,2},{4,5},{5,4},{6,7},{7,6},{8,9},{9,8},{10,11... | collective-permute-start | bytes 663560 | tf_op jit(solution)/shard_map/ppermute | solution.py:250
where the time goes:
time: 87.9 us; the launch traced here: 88.9 us
  starting transfers between devices  42.4 us (48%)
  waiting for transfers between devices  16.4 us (19%)
  local copies, waits for them, and re-layouts  12.7 us (14%)
  Pallas kernels  12.2 us (14%)
  other arithmetic  3.42 us (4%)
  between operations  1.68 us (2%)
    ppermute x7, starting transfers between devices, step_to(): return lax.ppermute(x, 'space', pairs)  23.3 us
    ppermute x9, starting transfers between devices, swap(): return lax.ppermute(value, axis, [(i, i ^ reach) for i in range(size)])  19.1 us
    ppermute x9, waiting for transfers between devices, swap(): return lax.ppermute(value, axis, [(i, i ^ reach) for i in range(size)])  11.9 us
    pallas_call x1, Pallas kernels, shards(): pl.pallas_call(first_half, out_shape=(long_shape, side_shape, side_shape,...  5.43 us
    ppermute x7, waiting for transfers between devices, step_to(): return lax.ppermute(x, 'space', pairs)  4.53 us
    pallas_call x1, Pallas kernels, shards(): pl.pallas_call(second_half, out_shape=(shape(x.shape, bf16), shape(x.shap...  4.37 us
    reshape x4, local copies, waits for them, and re-layouts, turned(): return kernel.reshape(channels, taps, channels)[:, ::-1].reshape(channels...  3.42 us
    unnamed x21, local copies, waits for them, and re-layouts  2.52 us
  transfers between devices with their start and end apart: 16, of which 6 were waited for; matrix products, arithmetic and copies ran while one was open for 12% of the time, Pallas kernels for 5%

commit v1 on v0

--- a/solution.py
+++ b/solution.py
@@ -7,6 +7,7 @@
 from jax.experimental import pallas as pl
 from jax.experimental.pallas import tpu as pltpu
 from jax.sharding import PartitionSpec as P
+
 
 EDGE = 8
 WORK_CAP = 2
@@ -45,16 +46,58 @@
     return pltpu.roll(jnp.concatenate([values, tail], axis=1), PLANE, 1)
 
 
-def stage(x_ref, dy_ref, long_ref, last_ref, first_ref):
+def sides(x_first, x_last, dy_first, dy_last, last_ref, first_ref):
+    slots, channels = x_first.shape[0], x_first.shape[1]
+    front = lax.broadcasted_iota(jnp.int32, (channels, LANES), 1) < PLANE
+    for slot in range(slots):
+        for half, (begin, end) in enumerate(((x_first, x_last), (dy_first, dy_last))):
+            band = slice(half * channels, (half + 1) * channels)
+            late = pltpu.roll(end[slot].astype(jnp.float32), PLANE, 1)
+            last_ref[slot, band, :] = jnp.where(front, late, 0.0).astype(jnp.bfloat16)
+            early = pltpu.roll(begin[slot].astype(jnp.float32), PLANE, 1)
+            first_ref[slot, band, :] = jnp.where(front, 0.0, early).astype(jnp.bfloat16)
+
+
+def prepare(
+    x_ref, dy_ref, one_ref, two_ref, long_ref, one_straight, two_straight, one_turned, two_turned
+):
     slots, channels = x_ref.shape[0], x_ref.shape[1]
     for slot in range(slots):
         for half, ref in enumerate((x_ref, dy_ref)):
             long_ref[slot, half * channels : (half + 1) * channels, :] = shifted_right(
                 ref[slot].astype(jnp.float32)
             ).astype(jnp.bfloat16)
-        last_ref[slot] = long_ref[slot, :, LONG - LANES :]
-        first_ref[slot] = long_ref[slot, :, :LANES]
     long_ref[slots] = jnp.zeros(long_ref.shape[1:], jnp.bfloat16)
+    width = one_ref.shape[1]
+    third = width // 3
+    both = jnp.concatenate(
+        [one_ref[...].astype(jnp.float32), two_ref[...].astype(jnp.float32)], axis=0
+    )
+    for p in range(3):
+        part = both[:, p * third : (p + 1) * third].astype(jnp.bfloat16)
+        one_straight[p * channels : (p + 1) * channels, :] = part[:channels]
+        two_straight[p * channels : (p + 1) * channels, :] = part[channels:]
+    taps = width // channels
+    spare = -width % LANES
+    flipped = jnp.concatenate([both, jnp.zeros((2 * channels, spare), jnp.float32)], axis=1).T
+    front = lax.broadcasted_iota(jnp.int32, (channels, LANES), 1) < PLANE
+
+    def block(tap):
+        return flipped[tap * channels : (tap + 1) * channels, :]
+
+    for p in range(3):
+        band = slice(p * channels, (p + 1) * channels)
+        for start in range(0, 9, 2):
+            here = block(taps - 1 - (9 * p + start))
+            lanes = slice(start * channels, min(start + 2, 9) * channels)
+            if start + 1 < 9:
+                after = block(taps - 1 - (9 * p + start + 1))
+                one = jnp.where(front, here, pltpu.roll(after, PLANE, 1))
+                two = jnp.where(front, pltpu.roll(here, PLANE, 1), after)
+            else:
+                one, two = here[:, :channels], pltpu.roll(here, PLANE, 1)[:, :channels]
+            one_turned[band, lanes] = one.astype(jnp.bfloat16)
+            two_turned[band, lanes] = two.astype(jnp.bfloat16)
 
 
 def gather_sides(slots, low_ref, high_ref, low, high):
@@ -76,7 +119,7 @@
                 continue
             number = 9 * (p + 1) + 3 * (q + 1) + (r + 1)
             number = number if number < 13 else number - 1
-            found = link[number * slots + j]
+            found = link[j, number]
             place[p, q, r] = jnp.where(found < 0, slots, found)
     one = jnp.ones((16, LANES), jnp.bfloat16)
     for tile in range(LONG // LANES):
@@ -275,35 +318,34 @@
     taps = kernel_one.shape[1] // channels
     x, dy = features[0], cotangent[0]
     count = brick_count[0]
-    link = neighbours[0].reshape(-1)
+    link = neighbours[0].T
     bf16, f32 = jnp.bfloat16, jnp.float32
     shape = jax.ShapeDtypeStruct
     long_shape = shape((slots + 1, 2 * channels, LONG), bf16)
     side_shape = shape((slots, 2 * channels, LANES), bf16)
     moves, edges = turn_tables()
-
-    def straight(kernel):
-        return (
-            kernel.reshape(channels, 3, 9 * channels)
-            .transpose(1, 0, 2)
-            .reshape(3 * channels, 9 * channels)
-        )
-
-    def turned(kernel):
-        return (
-            kernel.reshape(channels, taps, channels)[:, ::-1]
-            .reshape(channels, 3, 9, channels)
-            .transpose(1, 3, 2, 0)
-            .reshape(3 * channels, 9 * channels)
-        )
-
-    long_in, last, first = pl.pallas_call(
-        stage,
-        out_shape=(long_shape, side_shape, side_shape),
-        in_specs=vmem(2),
-        out_specs=tuple(vmem(3)),
-        name="stage",
-    )(x, dy)
+    params = pltpu.CompilerParams(vmem_limit_bytes=20 * 2**20)
+
+    ends = [pl.BlockSpec((slots, channels, LANES), lambda i, at=at: (0, 0, at)) for at in (0, 3)]
+    whole = pl.BlockSpec((slots, 2 * channels, LANES), lambda i: (0, 0, 0))
+    last, first = pl.pallas_call(
+        sides,
+        grid=(1,),
+        out_shape=(side_shape, side_shape),
+        in_specs=ends + ends,
+        out_specs=(whole, whole),
+        compiler_params=params,
+        name="sides",
+    )(x, x, dy, dy)
+    weight_shape = shape((3 * channels, 9 * channels), bf16)
+    long_in, one_straight, two_straight, one_turned, two_turned = pl.pallas_call(
+        prepare,
+        out_shape=(long_shape,) + (weight_shape,) * 4,
+        in_specs=vmem(4),
+        out_specs=tuple(vmem(5)),
+        compiler_params=params,
+        name="prepare",
+    )(x, dy, kernel_one, kernel_two)
     low = step_to(last, 1, False)
     high = step_to(first, -1, False)
     side_scratch = pltpu.VMEM((slots + 1, 2 * channels, LANES), bf16)
@@ -328,8 +370,9 @@
             pltpu.VMEM((3 * channels, 9 * channels), f32),
             pltpu.VMEM((9 * channels, 3 * channels), f32),
         ],
+        compiler_params=params,
         name="first_half",
-    )(link, count, long_in, low, high, edges, moves, straight(kernel_one), turned(kernel_two))
+    )(link, count, long_in, low, high, edges, moves, one_straight, two_turned)
     inner_low = step_to(inner_last, 1, False)
     inner_high = step_to(inner_first, -1, False)
     out, grad_in = pl.pallas_call(
@@ -338,10 +381,10 @@
         in_specs=smem(2) + vmem(9),
         out_specs=tuple(vmem(2)),
         scratch_shapes=[side_scratch, side_scratch, mixed_scratch, field_scratch, field_scratch],
+        compiler_params=params,
         name="second_half",
     )(
-        link, count, inner, inner_low, inner_high, edges, moves,
-        straight(kernel_two), turned(kernel_one), x, dy,
+        link, count, inner, inner_low, inner_high, edges, moves, two_straight, one_turned, x, dy
     )
     arrived = jnp.zeros_like(out[0])
     for step in range(slots - WORK_CAP):
@@ -356,8 +399,12 @@
 
 
 def solution(mesh):
+    return whole_step(mesh, shards)
+
+
+def whole_step(mesh, step):
     return jax.shard_map(
-        shards,
+        step,
         mesh=mesh,
         in_specs=(
             P("batch", "space", None, None),

time: 87.9 us -> 82.8 us (0.942); the launches traced: 88.9 us -> 82 us
  Pallas kernels: 12.2 us -> 6.77 us
  local copies, waits for them, and re-layouts: 12.7 us -> 8.81 us
  waiting for transfers between devices: 16.4 us -> 18.2 us
  other arithmetic: 3.42 us -> 4.89 us
    unnamed x21 -> x35, local copies, waits for them, and re-layouts: 2.52 us -> 7.82 us
    reshape x8 -> x0, local copies, waits for them, and re-layouts: 4.73 us -> none  [the longest x4 3.42 us: turned(): return kernel.reshape(channels, taps, channels)[:, ::-1].reshape(channels...]
    ppermute x7, waiting for transfers between devices: 4.53 us -> 8.86 us  [step_to(): return lax.ppermute(x, 'space', pairs)]
    ppermute x7, starting transfers between devices: 23.3 us -> 20.1 us  [step_to(): return lax.ppermute(x, 'space', pairs)]
    ppermute x9, waiting for transfers between devices: 11.9 us -> 9.33 us  [swap(): return lax.ppermute(value, axis, [(i, i ^ reach) for i in range(size)])]
    ppermute x9, starting transfers between devices: 19.1 us -> 21.7 us  [swap(): return lax.ppermute(value, axis, [(i, i ^ reach) for i in range(size)])]
    pallas_call x1, Pallas kernels: 5.43 us -> 3.11 us  [shards(): pl.pallas_call(first_half, out_shape=(long_shape, side_shape, side_shape,...]
    add x4, other arithmetic: 0.13 us -> 2.31 us  [all_sum(): rows = keep + swap(give, axis, reach).astype(jnp.float32)]
  transfers between devices with their start and end apart: 16 -> 16, of which waited for: 6 -> 9; matrix products, arithmetic and copies ran while one was open for 12% -> 2% of each run, Pallas kernels for 5% -> 4%
where the time goes in v1:
time: 82.8 us; the launch traced here: 82 us
  starting transfers between devices  41.7 us (50%)
  waiting for transfers between devices  18.2 us (22%)
  local copies, waits for them, and re-layouts  8.81 us (11%)
  Pallas kernels  6.77 us (8%)
  other arithmetic  4.89 us (6%)
  between operations  1.59 us (2%)
    ppermute x9, starting transfers between devices, swap(): return lax.ppermute(value, axis, [(i, i ^ reach) for i in range(size)])  21.7 us
    ppermute x7, starting transfers between devices, step_to(): return lax.ppermute(x, 'space', pairs)  20.1 us
    ppermute x9, waiting for transfers between devices, swap(): return lax.ppermute(value, axis, [(i, i ^ reach) for i in range(size)])  9.33 us
    ppermute x7, waiting for transfers between devices, step_to(): return lax.ppermute(x, 'space', pairs)  8.86 us
    unnamed x35, local copies, waits for them, and re-layouts  7.82 us
    pallas_call x1, Pallas kernels, shards(): pl.pallas_call(first_half, out_shape=(long_shape, side_shape, side_shape,...  3.11 us
    pallas_call x1, Pallas kernels, shards(): pl.pallas_call(second_half, out_shape=(shape(x.shape, bf16), shape(x.shap...  2.9 us
    add x4, other arithmetic, all_sum(): rows = keep + swap(give, axis, reach).astype(jnp.float32)  2.31 us
  transfers between devices with their start and end apart: 16, of which 9 were waited for; matrix products, arithmetic and copies ran while one was open for 2% of the time, Pallas kernels for 4%

profile of v1, /device:TPU:1, one launch (start us, length us, event | category | flops | bytes accessed | tf_op | source)
XLA Modules:
  0.0 82.0 jit_solution(1188184115765858206)
XLA Ops:
  0.6 1.0 %copy-done = bf16[1,5,64,512]{3,2,1,0:T(8,128)(2,1)S(1)} copy-done((bf16[1,5,64,512]{3,2,1,0:T(8,128)(2,1)S(1)}, bf16[1,5,64,512]{3,2,1,0:T(8,128)(2,1)}, u32[]{:S(2)}) %copy-start) | copy-done | bytes 327704
  1.6 1.0 %copy-done.2 = bf16[1,5,64,512]{3,2,1,0:T(8,128)(2,1)S(1)} copy-done((bf16[1,5,64,512]{3,2,1,0:T(8,128)(2,1)S(1)}, bf16[1,5,64,512]{3,2,1,0:T(8,128)(2,1)}, u32[]{:S(2)}) %copy-start.2) | copy-done | bytes 327704
  2.6 0.2 sides.1
  2.8 4.6 %collective-permute-start = (bf16[5,128,128]{2,1,0:T(8,128)(2,1)S(1)}, bf16[5,128,128]{2,1,0:T(8,128)(2,1)S(1)}, u32[]{:S(2)}, u32[]{:S(2)}) collective-permute-start(bf16[5,128,128]{2,1,0:T(8,128)(2,1)S(1)} %get-tuple-element.18), channel_id=1, source_target_pairs={{0,1},{1,2},{2,3},{3,4},{4,5},{5,6},{6,7},{7,8},{8,9},{9,10},{10,1... | collective-permute-start | bytes 491528 | tf_op jit(solution)/shard_map/ppermute | solution.py:280
  7.4 1.9 %collective-permute-start.1 = (bf16[5,128,128]{2,1,0:T(8,128)(2,1)S(1)}, bf16[5,128,128]{2,1,0:T(8,128)(2,1)S(1)}, u32[]{:S(2)}, u32[]{:S(2)}) collective-permute-start(bf16[5,128,128]{2,1,0:T(8,128)(2,1)S(1)} %get-tuple-element.19), channel_id=1, source_target_pairs={{1,0},{2,1},{3,2},{4,3},{5,4},{6,5},{7,6},{8,7},{9,8},{10,9},{11,1... | collective-permute-start | bytes 491528 | tf_op jit(solution)/shard_map/ppermute | solution.py:280
  9.3 0.7 copy.14
  10.7 0.0 copy-start.8
  10.7 0.9 %copy-done.8 = bf16[64,1728]{1,0:T(8,128)(2,1)S(1)} copy-done((bf16[64,1728]{1,0:T(8,128)(2,1)S(1)}, bf16[64,1728]{1,0:T(8,128)(2,1)}, u32[]{:S(2)}) %copy-start.8) | copy-done | bytes 221208
  11.7 0.9 %copy-done.9 = bf16[64,1728]{1,0:T(8,128)(2,1)S(1)} copy-done((bf16[64,1728]{1,0:T(8,128)(2,1)S(1)}, bf16[64,1728]{1,0:T(8,128)(2,1)}, u32[]{:S(2)}) %copy-start.9) | copy-done | bytes 221208
  12.6 0.6 prepare.1
  13.2 0.0 collective-permute-done.low_ref
  13.2 0.8 %collective-permute-done.1.high_ref = bf16[5,128,128]{2,1,0:T(8,128)(2,1)S(1)} collective-permute-done((bf16[5,128,128]{2,1,0:T(8,128)(2,1)S(1)}, bf16[5,128,128]{2,1,0:T(8,128)(2,1)S(1)}, u32[]{:S(2)}, u32[]{:S(2)}) %collective-permute-start.1) | collective-permute-done | bytes 163872 | tf_op jit(solution)/shard_map/ppermute | solution.py:280
  14.0 0.7 copy-done.10
  14.7 0.9 %copy-done.11 = bf16[5,128,128]{2,1,0:T(8,128)(2,1)S(1)} copy-done((bf16[5,128,128]{2,1,0:T(8,128)(2,1)S(1)}, bf16[5,128,128]{2,1,0:T(8,128)(2,1)}, u32[]{:S(2)}) %copy-start.11) | copy-done | bytes 163864
  15.6 3.1 %first_half.1 = (bf16[6,128,640]{2,1,0:T(8,128)(2,1)S(1)}, bf16[5,128,128]{2,1,0:T(8,128)(2,1)S(1)}, bf16[5,128,128]{2,1,0:T(8,128)(2,1)S(1)}, f32[128,1728]{1,0:T(8,128)S(1)}) custom-call(s32[5,26]{1,0:T(8,128)S(1)} %bitcast.29, s32[1]{0:T(128)} %bitcast.19.count, bf16[6,128,640]{2,1,0:T(8,128)(2,1)S(1)} %get-tuple-element.17.long_ref, ...), custom_call_target="tpu_custom_call" | custom-call | tf_op jit(solution)/shard_map/first_half/pallas_call | solution.py:354
  18.8 0.9 %copy-done.5 = bf16[6,128,640]{2,1,0:T(8,128)(2,1)} copy-done((bf16[6,128,640]{2,1,0:T(8,128)(2,1)}, bf16[6,128,640]{2,1,0:T(8,128)(2,1)S(1)}, u32[]{:S(2)}) %copy-start.5) | copy-done | bytes 983064
  19.7 0.9 %slice_select_fusion = f32[64,1728]{1,0:T(8,128)} fusion(f32[128,1728]{1,0:T(8,128)S(1)} %get-tuple-element.29, pred[]{:T(512)S(6)} %eq.29), kind=kLoop, calls=%fused_computation.2 | loop fusion | flops 110592 | bytes 1327105 | tf_op jit(solution)/shard_map/jit(_where)/select_n | solution.py:302
  20.6 2.1 %collective-permute-done.7 = f32[64,1728]{1,0:T(8,128)} collective-permute-done((f32[64,1728]{1,0:T(8,128)}, f32[64,1728]{1,0:T(8,128)}, u32[]{:S(2)}, u32[]{:S(2)}) %collective-permute-start.7) | collective-permute-done | bytes 442400 | tf_op jit(solution)/shard_map/ppermute | solution.py:293
  22.7 1.1 %select_add_fusion = f32[64,1728]{1,0:T(8,128)S(1)} fusion(f32[64,1728]{1,0:T(8,128)} %collective-permute-done.7, f32[128,1728]{1,0:T(8,128)S(1)} %get-tuple-element.29, pred[]{:T(512)S(6)} %eq.29), kind=kLoop, calls=%fused_computation.1 | loop fusion | flops 221184 | bytes 1769473 | tf_op jit(solution)/shard_map/add | solution.py:303
  23.9 0.8 copy-done.16
  24.7 9.3 %collective-permute-start.8 = (bf16[32,1728]{1,0:T(8,128)(2,1)S(1)}, bf16[32,1728]{1,0:T(8,128)(2,1)}, u32[]{:S(2)}, u32[]{:S(2)}) collective-permute-start(bf16[32,1728]{1,0:T(8,128)(2,1)S(1)} %select_convert_fusion), channel_id=1, source_target_pairs={{0,2},{1,3},{2,0},{3,1},{4,6},{5,7},{6,4},{7,5},{8,10},{9,11},{10,... | collective-permute-start | bytes 331784 | tf_op jit(solution)/shard_map/ppermute | solution.py:293
  33.9 3.3 %collective-permute-done.8 = bf16[32,1728]{1,0:T(8,128)(2,1)} collective-permute-done((bf16[32,1728]{1,0:T(8,128)(2,1)S(1)}, bf16[32,1728]{1,0:T(8,128)(2,1)}, u32[]{:S(2)}, u32[]{:S(2)}) %collective-permute-start.8) | collective-permute-done | bytes 110624 | tf_op jit(solution)/shard_map/ppermute | solution.py:293
  37.2 1.1 %convert_add_fusion = f32[32,1728]{1,0:T(8,128)S(1)} fusion(bf16[32,1728]{1,0:T(8,128)(2,1)} %collective-permute-done.8, f32[64,1728]{1,0:T(8,128)} %copy-done.16, pred[]{:T(512)S(6)} %eq.30), kind=kLoop, calls=%fused_computation.4 | loop fusion | flops 165888 | bytes 774145 | tf_op jit(solution)/shard_map/add | solution.py:303
  38.3 0.6 select_convert_fusion.1
  39.0 1.3 %collective-permute-start.9 = (bf16[16,1728]{1,0:T(8,128)(2,1)}, bf16[16,1728]{1,0:T(8,128)(2,1)S(1)}, u32[]{:S(2)}, u32[]{:S(2)}) collective-permute-start(bf16[16,1728]{1,0:T(8,128)(2,1)} %select_convert_fusion.1), channel_id=1, source_target_pairs={{0,4},{1,5},{2,6},{3,7},{4,0},{5,1},{6,2},{7,3},{8,12},{9,13},{10,... | collective-permute-start | bytes 165896 | tf_op jit(solution)/shard_map/ppermute | solution.py:293
  40.3 1.9 %collective-permute-done.9 = bf16[16,1728]{1,0:T(8,128)(2,1)S(1)} collective-permute-done((bf16[16,1728]{1,0:T(8,128)(2,1)}, bf16[16,1728]{1,0:T(8,128)(2,1)S(1)}, u32[]{:S(2)}, u32[]{:S(2)}) %collective-permute-start.9) | collective-permute-done | bytes 55328 | tf_op jit(solution)/shard_map/ppermute | solution.py:293
  42.2 0.0 copy-start.15
  42.2 0.0 copy-start.13
  42.3 2.4 %collective-permute-start.10 = (f32[8,1728]{1,0:T(8,128)S(1)}, f32[8,1728]{1,0:T(8,128)S(1)}, u32[]{:S(2)}, u32[]{:S(2)}) collective-permute-start(f32[8,1728]{1,0:T(8,128)S(1)} %slice_select_fusion.1), channel_id=1, source_target_pairs={{0,8},{1,9},{2,10},{3,11},{4,12},{5,13},{6,14},{7,15},{8,0},{9,1},... | collective-permute-start | bytes 165896 | tf_op jit(solution)/shard_map/ppermute | solution.py:293
  44.6 1.6 %collective-permute-done.10 = f32[8,1728]{1,0:T(8,128)S(1)} collective-permute-done((f32[8,1728]{1,0:T(8,128)S(1)}, f32[8,1728]{1,0:T(8,128)S(1)}, u32[]{:S(2)}, u32[]{:S(2)}) %collective-permute-start.10) | collective-permute-done | bytes 55328 | tf_op jit(solution)/shard_map/ppermute | solution.py:293
  46.3 2.1 %collective-permute-start.11 = (f32[8,1728]{1,0:T(8,128)S(1)}, f32[8,1728]{1,0:T(8,128)S(1)}, u32[]{:S(2)}, u32[]{:S(2)}) collective-permute-start(f32[8,1728]{1,0:T(8,128)S(1)} %select_add_fusion.1), channel_id=1, source_target_pairs={{0,16},{16,0},{1,17},{17,1},{2,18},{18,2},{3,19},{19,3},{4,20},{20... | collective-permute-start | bytes 165896 | tf_op jit(solution)/shard_map/ppermute | solution.py:293
  48.4 5.4 %collective-permute-start.2 = (bf16[5,128,128]{2,1,0:T(8,128)(2,1)S(1)}, bf16[5,128,128]{2,1,0:T(8,128)(2,1)S(1)}, u32[]{:S(2)}, u32[]{:S(2)}) collective-permute-start(bf16[5,128,128]{2,1,0:T(8,128)(2,1)S(1)} %copy-done.15), channel_id=1, source_target_pairs={{0,1},{1,2},{2,3},{3,4},{4,5},{5,6},{6,7},{7,8},{8,9},{9,10},{10,1... | collective-permute-start | bytes 491528 | tf_op jit(solution)/shard_map/ppermute | solution.py:280
  53.7 1.9 %collective-permute-start.3 = (bf16[5,128,128]{2,1,0:T(8,128)(2,1)S(1)}, bf16[5,128,128]{2,1,0:T(8,128)(2,1)S(1)}, u32[]{:S(2)}, u32[]{:S(2)}) collective-permute-start(bf16[5,128,128]{2,1,0:T(8,128)(2,1)S(1)} %copy-done.13), channel_id=1, source_target_pairs={{1,0},{2,1},{3,2},{4,3},{5,4},{6,5},{7,6},{8,7},{9,8},{10,9},{11,1... | collective-permute-start | bytes 491528 | tf_op jit(solution)/shard_map/ppermute | solution.py:280
  55.7 2.5 %collective-permute-start.12 = (bf16[8,1728]{1,0:T(8,128)(2,1)S(1)}, bf16[8,1728]{1,0:T(8,128)(2,1)S(1)}, u32[]{:S(2)}, u32[]{:S(2)}) collective-permute-start(bf16[8,1728]{1,0:T(8,128)(2,1)S(1)} %add_convert_fusion), channel_id=1, source_target_pairs={{0,8},{1,9},{2,10},{3,11},{4,12},{5,13},{6,14},{7,15},{8,0},{9,1},... | collective-permute-start | bytes 82952 | tf_op jit(solution)/shard_map/ppermute | solution.py:293
  58.2 2.2 %collective-permute-done.3.high_ref = bf16[5,128,128]{2,1,0:T(8,128)(2,1)S(1)} collective-permute-done((bf16[5,128,128]{2,1,0:T(8,128)(2,1)S(1)}, bf16[5,128,128]{2,1,0:T(8,128)(2,1)S(1)}, u32[]{:S(2)}, u32[]{:S(2)}) %collective-permute-start.3) | collective-permute-done | bytes 163872 | tf_op jit(solution)/shard_map/ppermute | solution.py:280
  60.4 2.9 %second_half.1 = (bf16[5,64,512]{2,1,0:T(8,128)(2,1)S(1)}, bf16[5,64,512]{2,1,0:T(8,128)(2,1)}) custom-call(s32[5,26]{1,0:T(8,128)S(1)} %bitcast.30, s32[1]{0:T(128)} %bitcast.20.count, bf16[6,128,640]{2,1,0:T(8,128)(2,1)S(1)} %copy-done.6, bf16[5,128,128]{2,1,0:T(8,128)(2,1)S(1)} %collective-permute-done.2.low_ref, ...), custom_call_target="tpu_custom_call" | custom-call | tf_op jit(solution)/shard_map/second_half/pallas_call | solution.py:378
  63.3 1.5 %collective-permute-start.13 = (bf16[16,1728]{1,0:T(8,128)(2,1)S(1)}, bf16[16,1728]{1,0:T(8,128)(2,1)S(1)}, u32[]{:S(2)}, u32[]{:S(2)}) collective-permute-start(bf16[16,1728]{1,0:T(8,128)(2,1)S(1)} %pad_maximum_fusion.2), channel_id=1, source_target_pairs={{0,4},{1,5},{2,6},{3,7},{4,0},{5,1},{6,2},{7,3},{8,12},{9,13},{10,... | collective-permute-start | bytes 165896 | tf_op jit(solution)/shard_map/ppermute | solution.py:293
  64.8 1.8 %collective-permute-start.6 = (bf16[64,512]{1,0:T(8,128)(2,1)S(1)}, bf16[64,512]{1,0:T(8,128)(2,1)S(1)}, u32[]{:S(2)}, u32[]{:S(2)}) collective-permute-start(bf16[64,512]{1,0:T(8,128)(2,1)S(1)} %get-tuple-element.35), channel_id=1, source_target_pairs={{0,3},{1,4},{2,5},{3,6},{4,7},{5,8},{6,9},{7,10},{8,11},{9,12},{10... | collective-permute-start | bytes 196616 | tf_op jit(solution)/shard_map/ppermute | solution.py:280
  66.7 4.4 %collective-permute-start.4 = (bf16[64,512]{1,0:T(8,128)(2,1)S(1)}, bf16[64,512]{1,0:T(8,128)(2,1)S(1)}, u32[]{:S(2)}, u32[]{:S(2)}) collective-permute-start(bf16[64,512]{1,0:T(8,128)(2,1)S(1)} %get-tuple-element.36), channel_id=1, source_target_pairs={{0,1},{1,2},{2,3},{3,4},{4,5},{5,6},{6,7},{7,8},{8,9},{9,10},{10,1... | collective-permute-start | bytes 196616 | tf_op jit(solution)/shard_map/ppermute | solution.py:280
  71.2 1.3 %collective-permute-start.14 = (bf16[32,1728]{1,0:T(8,128)(2,1)S(1)}, bf16[32,1728]{1,0:T(8,128)(2,1)S(1)}, u32[]{:S(2)}, u32[]{:S(2)}) collective-permute-start(bf16[32,1728]{1,0:T(8,128)(2,1)S(1)} %pad_maximum_fusion.1), channel_id=1, source_target_pairs={{0,2},{1,3},{2,0},{3,1},{4,6},{5,7},{6,4},{7,5},{8,10},{9,11},{10,... | collective-permute-start | bytes 331784 | tf_op jit(solution)/shard_map/ppermute | solution.py:293
  72.4 3.5 %collective-permute-done.6 = bf16[64,512]{1,0:T(8,128)(2,1)S(1)} collective-permute-done((bf16[64,512]{1,0:T(8,128)(2,1)S(1)}, bf16[64,512]{1,0:T(8,128)(2,1)S(1)}, u32[]{:S(2)}, u32[]{:S(2)}) %collective-permute-start.6) | collective-permute-done | bytes 65568 | tf_op jit(solution)/shard_map/ppermute | solution.py:280
  75.9 2.3 %collective-permute-done.5 = bf16[64,512]{1,0:T(8,128)(2,1)S(1)} collective-permute-done((bf16[64,512]{1,0:T(8,128)(2,1)S(1)}, bf16[64,512]{1,0:T(8,128)(2,1)S(1)}, u32[]{:S(2)}, u32[]{:S(2)}) %collective-permute-start.5) | collective-permute-done | bytes 65568 | tf_op jit(solution)/shard_map/ppermute | solution.py:280
  78.3 1.4 %collective-permute-start.15 = (bf16[64,1728]{1,0:T(8,128)(2,1)S(1)}, bf16[64,1728]{1,0:T(8,128)(2,1)S(1)}, u32[]{:S(2)}, u32[]{:S(2)}) collective-permute-start(bf16[64,1728]{1,0:T(8,128)(2,1)S(1)} %pad_maximum_fusion), channel_id=1, source_target_pairs={{0,1},{1,0},{2,3},{3,2},{4,5},{5,4},{6,7},{7,6},{8,9},{9,8},{10,11... | collective-permute-start | bytes 663560 | tf_op jit(solution)/shard_map/ppermute | solution.py:293
  79.7 0.7 select_bitcast_fusion
  80.5 0.4 collective-permute-done.15
  80.9 0.1 broadcast_select_fusion.1
  80.9 0.1 convert_multiply_fusion
  81.0 1.0 %fusion = (f32[64,1728]{1,0:T(8,128)}, f32[64,1728]{1,0:T(8,128)}) fusion(f32[128,1728]{1,0:T(8,128)S(1)} %convert_multiply_fusion), kind=kLoop, calls=%fused_computation.28 | loop fusion | bytes 1769472 | tf_op jit(solution)/shard_map/slice | solution.py:398
  (45 shorter events, 0.3 us)
Async XLA Ops:
  0.6 1.0 %copy-start = (bf16[1,5,64,512]{3,2,1,0:T(8,128)(2,1)S(1)}, bf16[1,5,64,512]{3,2,1,0:T(8,128)(2,1)}, u32[]{:S(2)}) copy-start(bf16[1,5,64,512]{3,2,1,0:T(8,128)(2,1)} %param.9) | copy-start | bytes 983044
  1.6 1.0 %copy-start.2 = (bf16[1,5,64,512]{3,2,1,0:T(8,128)(2,1)S(1)}, bf16[1,5,64,512]{3,2,1,0:T(8,128)(2,1)}, u32[]{:S(2)}) copy-start(bf16[1,5,64,512]{3,2,1,0:T(8,128)(2,1)} %param.10) | copy-start | bytes 983044
  2.6 8.1 %copy-start.1 = (bf16[1,5,64,512]{3,2,1,0:T(8,128)(2,1)S(1)}, bf16[1,5,64,512]{3,2,1,0:T(8,128)(2,1)}, u32[]{:S(2)}) copy-start(bf16[1,5,64,512]{3,2,1,0:T(8,128)(2,1)} %param.9) | copy-start | bytes 983044
  2.6 8.1 %copy-start.3 = (bf16[1,5,64,512]{3,2,1,0:T(8,128)(2,1)S(1)}, bf16[1,5,64,512]{3,2,1,0:T(8,128)(2,1)}, u32[]{:S(2)}) copy-start(bf16[1,5,64,512]{3,2,1,0:T(8,128)(2,1)} %param.10) | copy-start | bytes 983044
  2.6 12.1 %copy-start.4 = (bf16[8,256,256]{2,1,0:T(8,128)(2,1)S(1)}, bf16[8,256,256]{2,1,0:T(8,128)(2,1)}, u32[]{:S(2)}) copy-start(bf16[8,256,256]{2,1,0:T(8,128)(2,1)} %constant.75.clone.move_ref) | copy-start | bytes 3145732
  2.8 10.4 %collective-permute-start = (bf16[5,128,128]{2,1,0:T(8,128)(2,1)S(1)}, bf16[5,128,128]{2,1,0:T(8,128)(2,1)S(1)}, u32[]{:S(2)}, u32[]{:S(2)}) collective-permute-start(bf16[5,128,128]{2,1,0:T(8,128)(2,1)S(1)} %get-tuple-element.18), channel_id=1, source_target_pairs={{0,1},{1,2},{2,3},{3,4},{4,5},{5,6},{6,7},{7,8},{8,9},{9,10},{10,1... | collective-permute-start | bytes 491528 | tf_op jit(solution)/shard_map/ppermute | solution.py:280
  7.4 6.6 %collective-permute-start.1 = (bf16[5,128,128]{2,1,0:T(8,128)(2,1)S(1)}, bf16[5,128,128]{2,1,0:T(8,128)(2,1)S(1)}, u32[]{:S(2)}, u32[]{:S(2)}) collective-permute-start(bf16[5,128,128]{2,1,0:T(8,128)(2,1)S(1)} %get-tuple-element.19), channel_id=1, source_target_pairs={{1,0},{2,1},{3,2},{4,3},{5,4},{6,5},{7,6},{8,7},{9,8},{10,9},{11,1... | collective-permute-start | bytes 491528 | tf_op jit(solution)/shard_map/ppermute | solution.py:280
  10.7 0.9 %copy-start.8 = (bf16[64,1728]{1,0:T(8,128)(2,1)S(1)}, bf16[64,1728]{1,0:T(8,128)(2,1)}, u32[]{:S(2)}) copy-start(bf16[64,1728]{1,0:T(8,128)(2,1)} %one_ref.1) | copy-start | bytes 663556
  11.7 0.9 %copy-start.9 = (bf16[64,1728]{1,0:T(8,128)(2,1)S(1)}, bf16[64,1728]{1,0:T(8,128)(2,1)}, u32[]{:S(2)}) copy-start(bf16[64,1728]{1,0:T(8,128)(2,1)} %two_ref.1) | copy-start | bytes 663556
  12.6 2.1 %copy-start.7 = (bf16[4,16,640]{2,1,0:T(8,128)(2,1)S(1)}, bf16[4,16,640]{2,1,0:T(8,128)(2,1)}, u32[]{:S(2)}) copy-start(bf16[4,16,640]{2,1,0:T(8,128)(2,1)} %constant.76.clone.edge_ref) | copy-start | bytes 245764
  14.0 0.7 copy-start.10
  14.7 0.9 %copy-start.11 = (bf16[5,128,128]{2,1,0:T(8,128)(2,1)S(1)}, bf16[5,128,128]{2,1,0:T(8,128)(2,1)}, u32[]{:S(2)}) copy-start(bf16[5,128,128]{2,1,0:T(8,128)(2,1)} %copy-done.10) | copy-start | bytes 491524
  18.8 0.9 %copy-start.5 = (bf16[6,128,640]{2,1,0:T(8,128)(2,1)}, bf16[6,128,640]{2,1,0:T(8,128)(2,1)S(1)}, u32[]{:S(2)}) copy-start(bf16[6,128,640]{2,1,0:T(8,128)(2,1)S(1)} %get-tuple-element.22.inner_ref) | copy-start | bytes 2949124
  19.7 0.9 %copy-start.12 = (bf16[5,128,128]{2,1,0:T(8,128)(2,1)}, bf16[5,128,128]{2,1,0:T(8,128)(2,1)S(1)}, u32[]{:S(2)}) copy-start(bf16[5,128,128]{2,1,0:T(8,128)(2,1)S(1)} %get-tuple-element.24) | copy-start | bytes 491524
  19.7 0.9 %copy-start.14 = (bf16[5,128,128]{2,1,0:T(8,128)(2,1)}, bf16[5,128,128]{2,1,0:T(8,128)(2,1)S(1)}, u32[]{:S(2)}) copy-start(bf16[5,128,128]{2,1,0:T(8,128)(2,1)S(1)} %get-tuple-element.23) | copy-start | bytes 491524
  20.6 2.2 %collective-permute-start.7 = (f32[64,1728]{1,0:T(8,128)}, f32[64,1728]{1,0:T(8,128)}, u32[]{:S(2)}, u32[]{:S(2)}) collective-permute-start(f32[64,1728]{1,0:T(8,128)} %slice_select_fusion), channel_id=1, source_target_pairs={{0,1},{1,0},{2,3},{3,2},{4,5},{5,4},{6,7},{7,6},{8,9},{9,8},{10,11... | collective-permute-start | bytes 1327112 | tf_op jit(solution)/shard_map/ppermute | solution.py:293
  23.9 0.8 copy-start.16
  24.7 12.5 %collective-permute-start.8 = (bf16[32,1728]{1,0:T(8,128)(2,1)S(1)}, bf16[32,1728]{1,0:T(8,128)(2,1)}, u32[]{:S(2)}, u32[]{:S(2)}) collective-permute-start(bf16[32,1728]{1,0:T(8,128)(2,1)S(1)} %select_convert_fusion), channel_id=1, source_target_pairs={{0,2},{1,3},{2,0},{3,1},{4,6},{5,7},{6,4},{7,5},{8,10},{9,11},{10,... | collective-permute-start | bytes 331784 | tf_op jit(solution)/shard_map/ppermute | solution.py:293
  33.9 26.4 %copy-start.6 = (bf16[6,128,640]{2,1,0:T(8,128)(2,1)S(1)}, bf16[6,128,640]{2,1,0:T(8,128)(2,1)}, u32[]{:S(2)}) copy-start(bf16[6,128,640]{2,1,0:T(8,128)(2,1)} %copy-done.5) | copy-start | bytes 2949124
  39.0 3.2 %collective-permute-start.9 = (bf16[16,1728]{1,0:T(8,128)(2,1)}, bf16[16,1728]{1,0:T(8,128)(2,1)S(1)}, u32[]{:S(2)}, u32[]{:S(2)}) collective-permute-start(bf16[16,1728]{1,0:T(8,128)(2,1)} %select_convert_fusion.1), channel_id=1, source_target_pairs={{0,4},{1,5},{2,6},{3,7},{4,0},{5,1},{6,2},{7,3},{8,12},{9,13},{10,... | collective-permute-start | bytes 165896 | tf_op jit(solution)/shard_map/ppermute | solution.py:293
  42.2 6.1 %copy-start.15 = (bf16[5,128,128]{2,1,0:T(8,128)(2,1)S(1)}, bf16[5,128,128]{2,1,0:T(8,128)(2,1)}, u32[]{:S(2)}) copy-start(bf16[5,128,128]{2,1,0:T(8,128)(2,1)} %copy-done.14) | copy-start | bytes 491524
  42.2 11.5 %copy-start.13 = (bf16[5,128,128]{2,1,0:T(8,128)(2,1)S(1)}, bf16[5,128,128]{2,1,0:T(8,128)(2,1)}, u32[]{:S(2)}) copy-start(bf16[5,128,128]{2,1,0:T(8,128)(2,1)} %copy-done.12) | copy-start | bytes 491524
  42.3 4.0 %collective-permute-start.10 = (f32[8,1728]{1,0:T(8,128)S(1)}, f32[8,1728]{1,0:T(8,128)S(1)}, u32[]{:S(2)}, u32[]{:S(2)}) collective-permute-start(f32[8,1728]{1,0:T(8,128)S(1)} %slice_select_fusion.1), channel_id=1, source_target_pairs={{0,8},{1,9},{2,10},{3,11},{4,12},{5,13},{6,14},{7,15},{8,0},{9,1},... | collective-permute-start | bytes 165896 | tf_op jit(solution)/shard_map/ppermute | solution.py:293
  46.3 9.4 %collective-permute-start.11 = (f32[8,1728]{1,0:T(8,128)S(1)}, f32[8,1728]{1,0:T(8,128)S(1)}, u32[]{:S(2)}, u32[]{:S(2)}) collective-permute-start(f32[8,1728]{1,0:T(8,128)S(1)} %select_add_fusion.1), channel_id=1, source_target_pairs={{0,16},{16,0},{1,17},{17,1},{2,18},{18,2},{3,19},{19,3},{4,20},{20... | collective-permute-start | bytes 165896 | tf_op jit(solution)/shard_map/ppermute | solution.py:293
  48.4 9.8 %collective-permute-start.2 = (bf16[5,128,128]{2,1,0:T(8,128)(2,1)S(1)}, bf16[5,128,128]{2,1,0:T(8,128)(2,1)S(1)}, u32[]{:S(2)}, u32[]{:S(2)}) collective-permute-start(bf16[5,128,128]{2,1,0:T(8,128)(2,1)S(1)} %copy-done.15), channel_id=1, source_target_pairs={{0,1},{1,2},{2,3},{3,4},{4,5},{5,6},{6,7},{7,8},{8,9},{9,10},{10,1... | collective-permute-start | bytes 491528 | tf_op jit(solution)/shard_map/ppermute | solution.py:280
  53.7 6.6 %collective-permute-start.3 = (bf16[5,128,128]{2,1,0:T(8,128)(2,1)S(1)}, bf16[5,128,128]{2,1,0:T(8,128)(2,1)S(1)}, u32[]{:S(2)}, u32[]{:S(2)}) collective-permute-start(bf16[5,128,128]{2,1,0:T(8,128)(2,1)S(1)} %copy-done.13), channel_id=1, source_target_pairs={{1,0},{2,1},{3,2},{4,3},{5,4},{6,5},{7,6},{8,7},{9,8},{10,9},{11,1... | collective-permute-start | bytes 491528 | tf_op jit(solution)/shard_map/ppermute | solution.py:280
  55.7 7.6 %collective-permute-start.12 = (bf16[8,1728]{1,0:T(8,128)(2,1)S(1)}, bf16[8,1728]{1,0:T(8,128)(2,1)S(1)}, u32[]{:S(2)}, u32[]{:S(2)}) collective-permute-start(bf16[8,1728]{1,0:T(8,128)(2,1)S(1)} %add_convert_fusion), channel_id=1, source_target_pairs={{0,8},{1,9},{2,10},{3,11},{4,12},{5,13},{6,14},{7,15},{8,0},{9,1},... | collective-permute-start | bytes 82952 | tf_op jit(solution)/shard_map/ppermute | solution.py:293
  63.3 7.8 %collective-permute-start.13 = (bf16[16,1728]{1,0:T(8,128)(2,1)S(1)}, bf16[16,1728]{1,0:T(8,128)(2,1)S(1)}, u32[]{:S(2)}, u32[]{:S(2)}) collective-permute-start(bf16[16,1728]{1,0:T(8,128)(2,1)S(1)} %pad_maximum_fusion.2), channel_id=1, source_target_pairs={{0,4},{1,5},{2,6},{3,7},{4,0},{5,1},{6,2},{7,3},{8,12},{9,13},{10,... | collective-permute-start | bytes 165896 | tf_op jit(solution)/shard_map/ppermute | solution.py:293
  64.8 11.1 %collective-permute-start.6 = (bf16[64,512]{1,0:T(8,128)(2,1)S(1)}, bf16[64,512]{1,0:T(8,128)(2,1)S(1)}, u32[]{:S(2)}, u32[]{:S(2)}) collective-permute-start(bf16[64,512]{1,0:T(8,128)(2,1)S(1)} %get-tuple-element.35), channel_id=1, source_target_pairs={{0,3},{1,4},{2,5},{3,6},{4,7},{5,8},{6,9},{7,10},{8,11},{9,12},{10... | collective-permute-start | bytes 196616 | tf_op jit(solution)/shard_map/ppermute | solution.py:280
  66.7 9.2 %collective-permute-start.4 = (bf16[64,512]{1,0:T(8,128)(2,1)S(1)}, bf16[64,512]{1,0:T(8,128)(2,1)S(1)}, u32[]{:S(2)}, u32[]{:S(2)}) collective-permute-start(bf16[64,512]{1,0:T(8,128)(2,1)S(1)} %get-tuple-element.36), channel_id=1, source_target_pairs={{0,1},{1,2},{2,3},{3,4},{4,5},{5,6},{6,7},{7,8},{8,9},{9,10},{10,1... | collective-permute-start | bytes 196616 | tf_op jit(solution)/shard_map/ppermute | solution.py:280
  71.1 7.1 %collective-permute-start.5 = (bf16[64,512]{1,0:T(8,128)(2,1)S(1)}, bf16[64,512]{1,0:T(8,128)(2,1)S(1)}, u32[]{:S(2)}, u32[]{:S(2)}) collective-permute-start(bf16[64,512]{1,0:T(8,128)(2,1)S(1)} %get-tuple-element.34), channel_id=1, source_target_pairs={{0,2},{1,3},{2,4},{3,5},{4,6},{5,7},{6,8},{7,9},{8,10},{9,11},{10,... | collective-permute-start | bytes 196616 | tf_op jit(solution)/shard_map/ppermute | solution.py:280
  71.2 7.1 %collective-permute-start.14 = (bf16[32,1728]{1,0:T(8,128)(2,1)S(1)}, bf16[32,1728]{1,0:T(8,128)(2,1)S(1)}, u32[]{:S(2)}, u32[]{:S(2)}) collective-permute-start(bf16[32,1728]{1,0:T(8,128)(2,1)S(1)} %pad_maximum_fusion.1), channel_id=1, source_target_pairs={{0,2},{1,3},{2,0},{3,1},{4,6},{5,7},{6,4},{7,5},{8,10},{9,11},{10,... | collective-permute-start | bytes 331784 | tf_op jit(solution)/shard_map/ppermute | solution.py:293
  78.3 2.5 %collective-permute-start.15 = (bf16[64,1728]{1,0:T(8,128)(2,1)S(1)}, bf16[64,1728]{1,0:T(8,128)(2,1)S(1)}, u32[]{:S(2)}, u32[]{:S(2)}) collective-permute-start(bf16[64,1728]{1,0:T(8,128)(2,1)S(1)} %pad_maximum_fusion), channel_id=1, source_target_pairs={{0,1},{1,0},{2,3},{3,2},{4,5},{5,4},{6,7},{7,6},{8,9},{9,8},{10,11... | collective-permute-start | bytes 663560 | tf_op jit(solution)/shard_map/ppermute | solution.py:293

commit v2 on v1

--- a/solution.py
+++ b/solution.py
@@ -1,4 +1,5 @@
 import math
+from functools import partial
 
 import jax
 import jax.numpy as jnp
@@ -46,21 +47,43 @@
     return pltpu.roll(jnp.concatenate([values, tail], axis=1), PLANE, 1)
 
 
-def sides(x_first, x_last, dy_first, dy_last, last_ref, first_ref):
-    slots, channels = x_first.shape[0], x_first.shape[1]
+def sides(x_ref, dy_ref, last_ref, first_ref, begin, end, sems):
+    slots, channels = x_ref.shape[0], x_ref.shape[1]
+    copies = []
+    for half, ref in enumerate((x_ref, dy_ref)):
+        for number, (box, at) in enumerate(((begin, 0), (end, CELLS - LANES))):
+            copies.append(
+                pltpu.make_async_copy(
+                    ref.at[:, :, pl.ds(at, LANES)], box.at[half], sems.at[half, number]
+                )
+            )
+    for copy in copies:
+        copy.start()
+    for copy in copies:
+        copy.wait()
     front = lax.broadcasted_iota(jnp.int32, (channels, LANES), 1) < PLANE
     for slot in range(slots):
-        for half, (begin, end) in enumerate(((x_first, x_last), (dy_first, dy_last))):
+        for half in range(2):
             band = slice(half * channels, (half + 1) * channels)
-            late = pltpu.roll(end[slot].astype(jnp.float32), PLANE, 1)
+            late = pltpu.roll(end[half, slot].astype(jnp.float32), PLANE, 1)
             last_ref[slot, band, :] = jnp.where(front, late, 0.0).astype(jnp.bfloat16)
-            early = pltpu.roll(begin[slot].astype(jnp.float32), PLANE, 1)
+            early = pltpu.roll(begin[half, slot].astype(jnp.float32), PLANE, 1)
             first_ref[slot, band, :] = jnp.where(front, 0.0, early).astype(jnp.bfloat16)
 
 
 def prepare(
-    x_ref, dy_ref, one_ref, two_ref, long_ref, one_straight, two_straight, one_turned, two_turned
+    x_far, dy_far, one_far, two_far,
+    long_ref, one_straight, two_straight, one_turned, two_turned,
+    x_ref, dy_ref, one_ref, two_ref, sems,
 ):
+    pairs = ((x_far, x_ref), (dy_far, dy_ref), (one_far, one_ref), (two_far, two_ref))
+    copies = [
+        pltpu.make_async_copy(far, near, sems.at[k]) for k, (far, near) in enumerate(pairs)
+    ]
+    for copy in copies:
+        copy.start()
+    for copy in copies:
+        copy.wait()
     slots, channels = x_ref.shape[0], x_ref.shape[1]
     for slot in range(slots):
         for half, ref in enumerate((x_ref, dy_ref)):
@@ -119,7 +142,7 @@
                 continue
             number = 9 * (p + 1) + 3 * (q + 1) + (r + 1)
             number = number if number < 13 else number - 1
-            found = link[j, number]
+            found = link[j, 0, number]
             place[p, q, r] = jnp.where(found < 0, slots, found)
     one = jnp.ones((16, LANES), jnp.bfloat16)
     for tile in range(LONG // LANES):
@@ -188,8 +211,8 @@
 
 def first_half(
     link, count, long_ref, low_ref, high_ref, edge_ref, move_ref, one_ref, two_ref,
-    inner_ref, last_ref, first_ref, grad_ref,
-    low, high, mixed, field_x, field_dy, sum_one, sum_two,
+    inner_ref, last_ref, first_ref, keep_ref, give_ref,
+    low, high, mixed, field_x, field_dy, sum_one, sum_two, *, levels,
 ):
     slots = low_ref.shape[0]
     channels = long_ref.shape[1] // 2
@@ -225,31 +248,91 @@
         )
         return carry
 
-    lax.fori_loop(0, count[0], visit, 0)
+    lax.fori_loop(0, count[0, 0], visit, 0)
     for slot in range(slots):
         last_ref[slot] = inner_ref[slot, :, LONG - LANES :]
         first_ref[slot] = inner_ref[slot, :, :LANES]
-    grad_ref[:channels, :] = jnp.concatenate(
-        [sum_one[p * channels : (p + 1) * channels, :] for p in range(3)], axis=1
-    )
-    blocks = []
-    for tap in range(27):
-        p, rest = divmod(26 - tap, 9)
-        blocks.append(
-            sum_two[rest * channels : (rest + 1) * channels, p * channels : (p + 1) * channels]
+    halves = [keep_ref, give_ref]
+    upper = spot(levels[:1]) == 1
+
+    def write(one_ref, two_ref):
+        one_ref[...] = jnp.concatenate(
+            [sum_one[p * channels : (p + 1) * channels, :] for p in range(3)], axis=1
         )
-    grad_ref[channels:, :] = jnp.concatenate(blocks, axis=1)
-
-
-def second_half(
-    link, count, inner_ref, low_ref, high_ref, edge_ref, move_ref, two_ref, one_ref, x_ref, dy_ref,
-    out_ref, back_ref,
-    low, high, mixed, field_h, field_g,
-):
+        blocks = []
+        for tap in range(27):
+            p, rest = divmod(26 - tap, 9)
+            blocks.append(
+                sum_two[rest * channels : (rest + 1) * channels, p * channels : (p + 1) * channels]
+            )
+        two_ref[...] = jnp.concatenate(blocks, axis=1)
+
+    @pl.when(jnp.logical_not(upper))
+    def _():
+        write(*halves)
+
+    @pl.when(upper)
+    def _():
+        write(*halves[::-1])
+
+
+def spot(levels):
+    place = 0
+    for k, (axis, reach) in enumerate(levels):
+        place = place + (lax.axis_index(axis) // reach) % 2 * 2**k
+    return place
+
+
+def scatter(keep_ref, got_ref, *refs, levels):
+    *outs, total_ref = refs
+    total_ref[...] = keep_ref[...] + got_ref[...]
+    rows = outs[0].shape[0]
+    mine = spot(levels)
+    for k, out in enumerate(outs):
+        start = pl.multiple_of((mine ^ k) * rows, 16)
+        out[...] = total_ref[pl.ds(start, rows), :].astype(out.dtype)
+
+
+def paired_sum(*refs):
+    *parts, out_ref = refs
+    parts = [part[...].astype(jnp.float32) for part in parts]
+    while len(parts) > 1:
+        parts = [first + second for first, second in zip(parts[::2], parts[1::2])]
+    out_ref[...] = parts[0].astype(out_ref.dtype)
+
+
+def gather(*refs, levels):
+    *parts, out_ref = refs
+    rows = parts[0].shape[0]
+    mine = spot(levels)
+    for k, part in enumerate(parts):
+        out_ref[pl.ds(pl.multiple_of((mine ^ k) * rows, 16), rows), :] = part[...]
+
+
+def join_last(mine_ref, other_ref, one_ref, two_ref, *, levels, scale):
+    upper = spot(levels) == 1
+    mine = mine_ref[...].astype(jnp.float32) * scale
+    other = other_ref[...].astype(jnp.float32) * scale
+    one_ref[...] = jnp.where(upper, other, mine)
+    two_ref[...] = jnp.where(upper, mine, other)
+
+
+def place(count, *refs):
+    out_ref = refs[-1]
+    arrived = refs[1][...]
+    for ref in refs[2:-1]:
+        arrived = arrived + ref[...]
+    for slot in range(out_ref.shape[0]):
+        out_ref[slot] = jnp.where(count[0, 0] == slot, arrived, refs[0][slot])
+
+
+def second_half(begin, end, refs, scratch, out_ref, back_ref):
+    link, count, inner_ref, low_ref, high_ref, edge_ref, move_ref, two_ref, one_ref, x_ref, dy_ref = (
+        refs
+    )
+    low, high, mixed, field_h, field_g = scratch
     slots = low_ref.shape[0]
     gather_sides(slots, low_ref, high_ref, low, high)
-    out_ref[...] = jnp.zeros_like(out_ref)
-    back_ref[...] = jnp.zeros_like(back_ref)
 
     def visit(j, carry):
         spread(
@@ -257,13 +340,31 @@
         )
         out = convolved(two_ref, field_h)
         back = convolved(one_ref, field_g).astype(jnp.bfloat16)
-        out_ref[j] = (x_ref[j].astype(jnp.float32) + out).astype(jnp.bfloat16)
-        back_ref[j] = (dy_ref[j].astype(jnp.float32) + back.astype(jnp.float32)).astype(
+        out_ref[j - begin] = (x_ref[j].astype(jnp.float32) + out).astype(jnp.bfloat16)
+        back_ref[j - begin] = (dy_ref[j].astype(jnp.float32) + back.astype(jnp.float32)).astype(
             jnp.bfloat16
         )
         return carry
 
-    lax.fori_loop(0, count[0], visit, 0)
+    lax.fori_loop(begin, jnp.minimum(count[0, 0], end), visit, 0)
+
+
+def second_surplus(*refs):
+    slots = refs[3].shape[0]
+    inputs, back_ref, (*moved, out), scratch = refs[:11], refs[11], refs[12:-5], refs[-5:]
+    out[...] = jnp.zeros_like(out)
+    back_ref[...] = jnp.zeros_like(back_ref)
+    second_half(WORK_CAP, slots, inputs, scratch, out, back_ref)
+    for number, ref in enumerate(moved):
+        ref[...] = out[number]
+
+
+def second_own(*refs):
+    inputs, (part_ref, own_ref, back_ref), scratch = refs[:11], refs[11:14], refs[14:]
+    own_ref[...] = jnp.zeros_like(own_ref)
+    back_ref[:WORK_CAP] = jnp.zeros_like(own_ref)
+    back_ref[WORK_CAP:] = part_ref[...]
+    second_half(0, WORK_CAP, inputs, scratch, own_ref, back_ref)
 
 
 def vmem(count):
@@ -280,45 +381,74 @@
     return lax.ppermute(x, "space", pairs)
 
 
-def all_sum(rows):
-    levels = []
-    for axis in ("space", "batch"):
-        reach = 1
-        while reach < lax.axis_size(axis):
-            levels.append((axis, reach))
-            reach *= 2
-
-    def swap(value, axis, reach):
-        size = lax.axis_size(axis)
-        return lax.ppermute(value, axis, [(i, i ^ reach) for i in range(size)])
-
-    taken = []
-    for number, (axis, reach) in enumerate(levels):
-        wire = jnp.float32 if number == 0 or rows.shape[0] <= 16 else jnp.bfloat16
-        if rows.shape[0] > 8:
-            upper = (lax.axis_index(axis) // reach) % 2 == 1
-            middle = rows.shape[0] // 2
-            keep = jnp.where(upper, rows[middle:], rows[:middle])
-            give = jnp.where(upper, rows[:middle], rows[middle:]).astype(wire)
-            rows = keep + swap(give, axis, reach).astype(jnp.float32)
-            taken.append((axis, reach, upper))
-        else:
-            rows = rows + swap(rows, axis, reach)
-    rows = rows.astype(jnp.bfloat16)
-    for axis, reach, upper in taken[::-1]:
-        other = swap(rows, axis, reach)
-        rows = jnp.concatenate(
-            [jnp.where(upper, other, rows), jnp.where(upper, rows, other)], axis=0
-        )
-    return rows
+def groups_of():
+    levels = [
+        (axis, 2**k)
+        for axis in ("space", "batch")
+        for k in range(int(math.log2(lax.axis_size(axis))))
+    ]
+    rest = levels[2:-1]
+    pairs = [tuple(rest[k : k + 2]) for k in range(0, len(rest), 2)]
+    return [(levels[0],), (levels[1], levels[-1])] + pairs
+
+
+def all_sum(keep, give, groups, scale):
+    shape = jax.ShapeDtypeStruct
+    params = pltpu.CompilerParams(vmem_limit_bytes=6 * 2**20)
+    bf16 = jnp.bfloat16
+
+    def swap(value, levels, number):
+        reach = {"batch": 0, "space": 0}
+        for k, (axis, by) in enumerate(levels):
+            reach[axis] += by * (number >> k & 1)
+        width = lax.axis_size("space")
+        pairs = [
+            (i, ((i // width ^ reach["batch"]) * width) + (i % width ^ reach["space"]))
+            for i in range(lax.axis_size("batch") * width)
+        ]
+        return lax.ppermute(value, ("batch", "space"), pairs)
+
+    def call(body, outs, *arrays, scratch=(), **static):
+        outs = [shape(*out) for out in outs]
+        return pl.pallas_call(
+            partial(body, **static),
+            out_shape=outs,
+            in_specs=vmem(len(arrays)),
+            out_specs=vmem(len(outs)),
+            scratch_shapes=scratch,
+            compiler_params=params,
+        )(*arrays)
+
+    width = keep.shape[1]
+    whole = (keep.shape, jnp.float32)
+    pair, spread_over, *others = groups
+    got = swap(give, pair, 1)
+    members = 2 ** len(spread_over)
+    part = (keep.shape[0] // members, width)
+    mine, *gives = call(
+        scatter,
+        [(part, jnp.float32)] + [(part, bf16)] * (members - 1),
+        keep,
+        got,
+        levels=spread_over,
+        scratch=[pltpu.VMEM(keep.shape, jnp.float32)],
+    )
+    gots = [swap(value, spread_over, k + 1) for k, value in enumerate(gives)]
+    (mine,) = call(paired_sum, [(part, bf16)], mine, *gots)
+    for group in others:
+        gots = [swap(mine, group, k) for k in range(1, 2 ** len(group))]
+        (mine,) = call(paired_sum, [(part, bf16)], mine, *gots)
+    gots = [swap(mine, spread_over, k) for k in range(1, members)]
+    (mine,) = call(gather, [(keep.shape, bf16)], mine, *gots, levels=spread_over)
+    other = swap(mine, pair, 1)
+    return call(join_last, [whole, whole], mine, other, levels=pair, scale=scale)
 
 
 def shards(features, cotangent, brick_count, destination, neighbours, kernel_one, kernel_two):
     slots, channels = features.shape[1], features.shape[2]
-    taps = kernel_one.shape[1] // channels
     x, dy = features[0], cotangent[0]
-    count = brick_count[0]
-    link = neighbours[0].T
+    count = brick_count
+    link = neighbours.transpose(2, 0, 1)
     bf16, f32 = jnp.bfloat16, jnp.float32
     shape = jax.ShapeDtypeStruct
     long_shape = shape((slots + 1, 2 * channels, LONG), bf16)
@@ -326,23 +456,33 @@
     moves, edges = turn_tables()
     params = pltpu.CompilerParams(vmem_limit_bytes=20 * 2**20)
 
-    ends = [pl.BlockSpec((slots, channels, LANES), lambda i, at=at: (0, 0, at)) for at in (0, 3)]
-    whole = pl.BlockSpec((slots, 2 * channels, LANES), lambda i: (0, 0, 0))
+    far = pl.BlockSpec(memory_space=pltpu.HBM)
     last, first = pl.pallas_call(
         sides,
-        grid=(1,),
         out_shape=(side_shape, side_shape),
-        in_specs=ends + ends,
-        out_specs=(whole, whole),
+        in_specs=[far, far],
+        out_specs=tuple(vmem(2)),
+        scratch_shapes=[
+            pltpu.VMEM((2, slots, channels, LANES), bf16),
+            pltpu.VMEM((2, slots, channels, LANES), bf16),
+            pltpu.SemaphoreType.DMA((2, 2)),
+        ],
         compiler_params=params,
         name="sides",
-    )(x, x, dy, dy)
+    )(x, dy)
     weight_shape = shape((3 * channels, 9 * channels), bf16)
     long_in, one_straight, two_straight, one_turned, two_turned = pl.pallas_call(
         prepare,
         out_shape=(long_shape,) + (weight_shape,) * 4,
-        in_specs=vmem(4),
+        in_specs=[far] * 4,
         out_specs=tuple(vmem(5)),
+        scratch_shapes=[
+            pltpu.VMEM(x.shape, bf16),
+            pltpu.VMEM(x.shape, bf16),
+            pltpu.VMEM(kernel_one.shape, bf16),
+            pltpu.VMEM(kernel_one.shape, bf16),
+            pltpu.SemaphoreType.DMA((4,)),
+        ],
         compiler_params=params,
         name="prepare",
     )(x, dy, kernel_one, kernel_two)
@@ -351,16 +491,19 @@
     side_scratch = pltpu.VMEM((slots + 1, 2 * channels, LANES), bf16)
     mixed_scratch = pltpu.VMEM((len(TURNS), 2 * channels, LONG), bf16)
     field_scratch = pltpu.VMEM((9 * channels, LONG), bf16)
-    inner, inner_last, inner_first, grads = pl.pallas_call(
-        first_half,
+    groups = groups_of()
+    half_shape = shape(kernel_one.shape, f32)
+    inner, inner_last, inner_first, keep, give = pl.pallas_call(
+        partial(first_half, levels=groups[0]),
         out_shape=(
             long_shape,
             side_shape,
             side_shape,
-            shape((2 * channels, taps * channels), f32),
+            half_shape,
+            half_shape,
         ),
         in_specs=smem(2) + vmem(7),
-        out_specs=tuple(vmem(4)),
+        out_specs=tuple(vmem(5)),
         scratch_shapes=[
             side_scratch,
             side_scratch,
@@ -375,27 +518,47 @@
     )(link, count, long_in, low, high, edges, moves, one_straight, two_turned)
     inner_low = step_to(inner_last, 1, False)
     inner_high = step_to(inner_first, -1, False)
-    out, grad_in = pl.pallas_call(
-        second_half,
-        out_shape=(shape(x.shape, bf16), shape(x.shape, bf16)),
+    surplus = slots - WORK_CAP
+    brick = shape(x.shape[1:], bf16)
+    inputs = (
+        link, count, inner, inner_low, inner_high, edges, moves, two_straight, one_turned, x, dy
+    )
+    scratch = [side_scratch, side_scratch, mixed_scratch, field_scratch, field_scratch]
+    surplus_shape = (surplus,) + x.shape[1:]
+    part, *moved = pl.pallas_call(
+        second_surplus,
+        out_shape=(shape(surplus_shape, bf16),) + (brick,) * surplus,
         in_specs=smem(2) + vmem(9),
+        out_specs=tuple(vmem(1 + surplus)),
+        scratch_shapes=[pltpu.VMEM(surplus_shape, bf16)] + scratch,
+        compiler_params=params,
+        name="second_surplus",
+    )(*inputs)
+    own, grad_in = pl.pallas_call(
+        second_own,
+        out_shape=(shape((WORK_CAP,) + x.shape[1:], bf16), shape(x.shape, bf16)),
+        in_specs=smem(2) + vmem(10),
         out_specs=tuple(vmem(2)),
-        scratch_shapes=[side_scratch, side_scratch, mixed_scratch, field_scratch, field_scratch],
+        scratch_shapes=scratch,
         compiler_params=params,
-        name="second_half",
-    )(
-        link, count, inner, inner_low, inner_high, edges, moves, two_straight, one_turned, x, dy
-    )
-    arrived = jnp.zeros_like(out[0])
-    for step in range(slots - WORK_CAP):
-        arrived = arrived + step_to(out[WORK_CAP + step], step + 1, True)
-    free = (jnp.arange(WORK_CAP, dtype=jnp.int32) == count[0])[:, None, None]
-    placed = jnp.where(free, arrived[None], out[:WORK_CAP])
+        name="second_own",
+    )(*inputs, part)
+    arrived = []
+    for number, brick_out in enumerate(moved):
+        arrived.append(step_to(brick_out, number + 1, True))
+    placed = pl.pallas_call(
+        place,
+        out_shape=shape(own.shape, bf16),
+        in_specs=smem(1) + vmem(1 + surplus),
+        out_specs=pl.BlockSpec(memory_space=pltpu.VMEM),
+        compiler_params=params,
+        name="place",
+    )(count, own, *arrived)
     scale = 1.0 / math.sqrt(
         lax.axis_size("batch") * features.shape[0] * lax.axis_size("space") * slots * CELLS
     )
-    total = all_sum(grads).astype(f32) * scale
-    return (placed[None], grad_in[None], total[:channels], total[channels:])
+    grad_one, grad_two = all_sum(keep, give, groups, scale)
+    return (placed[None], grad_in[None], grad_one, grad_two)
 
 
 def solution(mesh):

time: 82.8 us -> 70.9 us (0.86)
  other arithmetic: 4.89 us -> 0 us
  local copies, waits for them, and re-layouts: 8.81 us -> 4.6 us
  Pallas kernels: 6.77 us -> 10.2 us
  starting transfers between devices: 41.7 us -> 38.7 us
  waiting for transfers between devices: 18.2 us -> 15.7 us
    ppermute x9 -> x11, starting transfers between devices: 21.7 us -> 17.6 us  [swap(): return lax.ppermute(value, ('batch', 'space'), pairs)]
    unnamed x35 -> x18, local copies, waits for them, and re-layouts: 7.82 us -> 4.6 us
    pallas_call x3 -> x10, Pallas kernels: 6.19 us -> 8.78 us  [the longest x1 3.14 us: shards(): pl.pallas_call(partial(first_half, levels=groups[0]), out_shape=(long_sha...]
    add x5 -> x0, other arithmetic: 2.32 us -> none  [the longest x4 2.31 us: all_sum(): rows = keep + swap(give, axis, reach).astype(jnp.float32)]
    ppermute x9 -> x11, waiting for transfers between devices: 9.33 us -> 7.24 us  [swap(): return lax.ppermute(value, ('batch', 'space'), pairs)]
    select_n x6 -> x0, other arithmetic: 1.04 us -> none  [the longest x2 0.88 us: all_sum(): give = jnp.where(upper, rows[:middle], rows[middle:]).astype(wire)]
    ppermute x7, starting transfers between devices: 20.1 us -> 21.1 us  [step_to(): return lax.ppermute(x, 'space', pairs)]
    slice x1 -> x0, local copies, waits for them, and re-layouts: 0.98 us -> none  [shards(): return (placed[None], grad_in[None], total[:channels], total[channels:])]
  transfers between devices with their start and end apart: 16 -> 18, of which waited for: 9 -> 12; matrix products, arithmetic and copies ran while one was open for 2% -> 0% of each run, Pallas kernels for 4% -> 8%
where the time goes in v2:
time: 70.9 us; the launch traced here: 70.6 us
  starting transfers between devices  38.7 us (55%)
  waiting for transfers between devices  15.7 us (22%)
  Pallas kernels  10.2 us (14%)
  local copies, waits for them, and re-layouts  4.6 us (6%)
  between operations  1.46 us (2%)
    ppermute x7, starting transfers between devices, step_to(): return lax.ppermute(x, 'space', pairs)  21.1 us
    ppermute x11, starting transfers between devices, swap(): return lax.ppermute(value, ('batch', 'space'), pairs)  17.6 us
    ppermute x7, waiting for transfers between devices, step_to(): return lax.ppermute(x, 'space', pairs)  8.42 us
    ppermute x11, waiting for transfers between devices, swap(): return lax.ppermute(value, ('batch', 'space'), pairs)  7.24 us
    unnamed x18, local copies, waits for them, and re-layouts  4.6 us
    pallas_call x1, Pallas kernels, shards(): pl.pallas_call(partial(first_half, levels=groups[0]), out_shape=(long_sha...  3.14 us
    pallas_call x1, Pallas kernels, shards(): pl.pallas_call(second_own, out_shape=(shape((WORK_CAP,) + x.shape[1:], bf...  2.88 us
  transfers between devices with their start and end apart: 18, of which 12 were waited for; matrix products, arithmetic and copies ran while one was open for 0% of the time, Pallas kernels for 8%

profile of v2, /device:TPU:1, one launch (start us, length us, event | category | flops | bytes accessed | tf_op | source)
XLA Modules:
  0.0 70.6 jit_solution(3101623641676832555)
XLA Ops:
  0.6 0.0 copy-start
  0.6 0.0 copy-start.1
  0.7 1.1 %copy-done.1 = bf16[1,5,64,512]{3,2,1,0:T(8,128)(2,1)S(1)} copy-done((bf16[1,5,64,512]{3,2,1,0:T(8,128)(2,1)S(1)}, bf16[1,5,64,512]{3,2,1,0:T(8,128)(2,1)}, u32[]{:S(2)}) %copy-start.1) | copy-done | bytes 327704
  1.7 1.0 %copy-done.3 = bf16[1,5,64,512]{3,2,1,0:T(8,128)(2,1)S(1)} copy-done((bf16[1,5,64,512]{3,2,1,0:T(8,128)(2,1)S(1)}, bf16[1,5,64,512]{3,2,1,0:T(8,128)(2,1)}, u32[]{:S(2)}) %copy-start.3) | copy-done | bytes 327704
  2.7 0.3 sides.1
  2.9 4.5 %collective-permute-start = (bf16[5,128,128]{2,1,0:T(8,128)(2,1)S(1)}, bf16[5,128,128]{2,1,0:T(8,128)(2,1)S(1)}, u32[]{:S(2)}, u32[]{:S(2)}) collective-permute-start(bf16[5,128,128]{2,1,0:T(8,128)(2,1)S(1)} %get-tuple-element.29), channel_id=1, source_target_pairs={{0,1},{1,2},{2,3},{3,4},{4,5},{5,6},{6,7},{7,8},{8,9},{9,10},{10,1... | collective-permute-start | bytes 491528 | tf_op jit(solution)/shard_map/ppermute | solution.py:381
  7.4 1.9 %collective-permute-start.1 = (bf16[5,128,128]{2,1,0:T(8,128)(2,1)S(1)}, bf16[5,128,128]{2,1,0:T(8,128)(2,1)S(1)}, u32[]{:S(2)}, u32[]{:S(2)}) collective-permute-start(bf16[5,128,128]{2,1,0:T(8,128)(2,1)S(1)} %get-tuple-element.30), channel_id=1, source_target_pairs={{1,0},{2,1},{3,2},{4,3},{5,4},{6,5},{7,6},{8,7},{9,8},{10,9},{11,1... | collective-permute-start | bytes 491528 | tf_op jit(solution)/shard_map/ppermute | solution.py:381
  10.0 0.0 copy-start.6
  10.0 0.9 %copy-done.6 = bf16[64,1728]{1,0:T(8,128)(2,1)S(1)} copy-done((bf16[64,1728]{1,0:T(8,128)(2,1)S(1)}, bf16[64,1728]{1,0:T(8,128)(2,1)}, u32[]{:S(2)}) %copy-start.6) | copy-done | bytes 221208
  11.0 0.9 %copy-done.7 = bf16[64,1728]{1,0:T(8,128)(2,1)S(1)} copy-done((bf16[64,1728]{1,0:T(8,128)(2,1)S(1)}, bf16[64,1728]{1,0:T(8,128)(2,1)}, u32[]{:S(2)}) %copy-start.7) | copy-done | bytes 221208
  11.9 1.4 %prepare.1 = (bf16[6,128,640]{2,1,0:T(8,128)(2,1)S(1)}, bf16[192,576]{1,0:T(8,128)(2,1)S(1)}, bf16[192,576]{1,0:T(8,128)(2,1)S(1)}, bf16[192,576]{1,0:T(8,128)(2,1)S(1)}, bf16[192,576]{1,0:T(8,128)(2,1)S(1)}) custom-call(bf16[5,64,512]{2,1,0:T(8,128)(2,1)S(1)} %bitcast.6, bf16[5,64,512]{2,1,0:T(8,128)(2,1)S(1)} %bitcast.10, bf16[64,1728]{1,0:T(8,128)(2,1)S(1)} %copy-done.6, ...), custom_call_target="tpu_custom_call" | custom-call | tf_op jit(solution)/shard_map/prepare/pallas_call | solution.py:474
  13.3 0.0 collective-permute-done.low_ref
  13.3 0.7 %collective-permute-done.1.high_ref = bf16[5,128,128]{2,1,0:T(8,128)(2,1)S(1)} collective-permute-done((bf16[5,128,128]{2,1,0:T(8,128)(2,1)S(1)}, bf16[5,128,128]{2,1,0:T(8,128)(2,1)S(1)}, u32[]{:S(2)}, u32[]{:S(2)}) %collective-permute-start.1) | collective-permute-done | bytes 163872 | tf_op jit(solution)/shard_map/ppermute | solution.py:381
  14.1 0.7 copy-done.8
  14.8 3.1 %first_half.1 = (bf16[6,128,640]{2,1,0:T(8,128)(2,1)S(1)}, bf16[5,128,128]{2,1,0:T(8,128)(2,1)S(1)}, bf16[5,128,128]{2,1,0:T(8,128)(2,1)S(1)}, f32[64,1728]{1,0:T(8,128)S(1)}, f32[64,1728]{1,0:T(8,128)S(1)}) custom-call(s32[5,1,26]{2,1,0:T(1,128)S(1)} %bitcast.13, s32[1,1]{1,0:T(1,128)S(6)} %copy.12.count.refs_1_, ...), custom_call_target="tpu_custom_call" | custom-call | tf_op jit(solution)/shard_map/first_half/pallas_call | solution.py:496
  17.9 0.1 collective-permute-start.7
  18.0 1.8 %collective-permute-done.7.got_ref = f32[64,1728]{1,0:T(8,128)S(1)} collective-permute-done((f32[64,1728]{1,0:T(8,128)S(1)}, f32[64,1728]{1,0:T(8,128)S(1)}, u32[]{:S(2)}, u32[]{:S(2)}) %collective-permute-start.7) | collective-permute-done | bytes 442400 | tf_op jit(solution)/shard_map/ppermute | solution.py:409
  19.8 0.1 shard_map.111
  19.9 9.4 %collective-permute-start.8 = (bf16[16,1728]{1,0:T(8,128)(2,1)S(1)}, bf16[16,1728]{1,0:T(8,128)(2,1)S(1)}, u32[]{:S(2)}, u32[]{:S(2)}) collective-permute-start(bf16[16,1728]{1,0:T(8,128)(2,1)S(1)} %get-tuple-element.47), channel_id=1, source_target_pairs={{0,2},{1,3},{2,0},{3,1},{4,6},{5,7},{6,4},{7,5},{8,10},{9,11},{10,... | collective-permute-start | bytes 165896 | tf_op jit(solution)/shard_map/ppermute | solution.py:409
  29.3 0.6 collective-permute-start.9
  29.9 1.1 %collective-permute-start.10 = (bf16[16,1728]{1,0:T(8,128)(2,1)S(1)}, bf16[16,1728]{1,0:T(8,128)(2,1)S(1)}, u32[]{:S(2)}, u32[]{:S(2)}) collective-permute-start(bf16[16,1728]{1,0:T(8,128)(2,1)S(1)} %get-tuple-element.49), channel_id=1, source_target_pairs={{0,18},{1,19},{2,16},{3,17},{4,22},{5,23},{6,20},{7,21},{8,26},{9,... | collective-permute-start | bytes 165896 | tf_op jit(solution)/shard_map/ppermute | solution.py:409
  31.0 0.2 collective-permute-done.8.refs_1_
  31.2 1.1 %collective-permute-done.9.refs_2_ = bf16[16,1728]{1,0:T(8,128)(2,1)S(1)} collective-permute-done((bf16[16,1728]{1,0:T(8,128)(2,1)S(1)}, bf16[16,1728]{1,0:T(8,128)(2,1)S(1)}, u32[]{:S(2)}, u32[]{:S(2)}) %collective-permute-start.9) | collective-permute-done | bytes 55328 | tf_op jit(solution)/shard_map/ppermute | solution.py:409
  32.3 1.6 %collective-permute-done.10.refs_3_ = bf16[16,1728]{1,0:T(8,128)(2,1)S(1)} collective-permute-done((bf16[16,1728]{1,0:T(8,128)(2,1)S(1)}, bf16[16,1728]{1,0:T(8,128)(2,1)S(1)}, u32[]{:S(2)}, u32[]{:S(2)}) %collective-permute-start.10) | collective-permute-done | bytes 55328 | tf_op jit(solution)/shard_map/ppermute | solution.py:409
  33.9 0.0 copy-start.2
  33.9 0.0 copy-start.4
  34.0 1.1 %collective-permute-start.13 = (bf16[16,1728]{1,0:T(8,128)(2,1)S(1)}, bf16[16,1728]{1,0:T(8,128)(2,1)S(1)}, u32[]{:S(2)}, u32[]{:S(2)}) collective-permute-start(bf16[16,1728]{1,0:T(8,128)(2,1)S(1)} %shard_map.112.refs_0_), channel_id=1, source_target_pairs={{0,12},{1,13},{2,14},{3,15},{4,8},{5,9},{6,10},{7,11},{8,4},{9,5},... | collective-permute-start | bytes 165896 | tf_op jit(solution)/shard_map/ppermute | solution.py:409
  35.1 1.4 %collective-permute-start.12 = (bf16[16,1728]{1,0:T(8,128)(2,1)S(1)}, bf16[16,1728]{1,0:T(8,128)(2,1)S(1)}, u32[]{:S(2)}, u32[]{:S(2)}) collective-permute-start(bf16[16,1728]{1,0:T(8,128)(2,1)S(1)} %shard_map.112.refs_0_), channel_id=1, source_target_pairs={{0,8},{1,9},{2,10},{3,11},{4,12},{5,13},{6,14},{7,15},{8,0},{9,1},... | collective-permute-start | bytes 165896 | tf_op jit(solution)/shard_map/ppermute | solution.py:409
  36.5 1.1 %collective-permute-start.11 = (bf16[16,1728]{1,0:T(8,128)(2,1)S(1)}, bf16[16,1728]{1,0:T(8,128)(2,1)S(1)}, u32[]{:S(2)}, u32[]{:S(2)}) collective-permute-start(bf16[16,1728]{1,0:T(8,128)(2,1)S(1)} %shard_map.112.refs_0_), channel_id=1, source_target_pairs={{0,4},{1,5},{2,6},{3,7},{4,0},{5,1},{6,2},{7,3},{8,12},{9,13},{10,... | collective-permute-start | bytes 165896 | tf_op jit(solution)/shard_map/ppermute | solution.py:409
  37.6 1.3 %collective-permute-done.13.refs_3_ = bf16[16,1728]{1,0:T(8,128)(2,1)S(1)} collective-permute-done((bf16[16,1728]{1,0:T(8,128)(2,1)S(1)}, bf16[16,1728]{1,0:T(8,128)(2,1)S(1)}, u32[]{:S(2)}, u32[]{:S(2)}) %collective-permute-start.13) | collective-permute-done | bytes 55328 | tf_op jit(solution)/shard_map/ppermute | solution.py:409
  38.9 0.7 collective-permute-done.12.refs_2_
  39.6 0.5 collective-permute-done.11.refs_1_
  40.1 1.2 %collective-permute-start.16 = (bf16[16,1728]{1,0:T(8,128)(2,1)S(1)}, bf16[16,1728]{1,0:T(8,128)(2,1)S(1)}, u32[]{:S(2)}, u32[]{:S(2)}) collective-permute-start(bf16[16,1728]{1,0:T(8,128)(2,1)S(1)} %shard_map.113.refs_0_), channel_id=1, source_target_pairs={{0,18},{1,19},{2,16},{3,17},{4,22},{5,23},{6,20},{7,21},{8,26},{9,... | collective-permute-start | bytes 165896 | tf_op jit(solution)/shard_map/ppermute | solution.py:409
  41.3 1.4 %collective-permute-start.15 = (bf16[16,1728]{1,0:T(8,128)(2,1)S(1)}, bf16[16,1728]{1,0:T(8,128)(2,1)S(1)}, u32[]{:S(2)}, u32[]{:S(2)}) collective-permute-start(bf16[16,1728]{1,0:T(8,128)(2,1)S(1)} %shard_map.113.refs_0_), channel_id=1, source_target_pairs={{0,16},{1,17},{2,18},{3,19},{4,20},{5,21},{6,22},{7,23},{8,24},{9,... | collective-permute-start | bytes 165896 | tf_op jit(solution)/shard_map/ppermute | solution.py:409
  42.6 0.2 collective-permute-start.14
  42.8 7.2 %collective-permute-start.2 = (bf16[5,128,128]{2,1,0:T(8,128)(2,1)S(1)}, bf16[5,128,128]{2,1,0:T(8,128)(2,1)S(1)}, u32[]{:S(2)}, u32[]{:S(2)}) collective-permute-start(bf16[5,128,128]{2,1,0:T(8,128)(2,1)S(1)} %get-tuple-element.34), channel_id=1, source_target_pairs={{0,1},{1,2},{2,3},{3,4},{4,5},{5,6},{6,7},{7,8},{8,9},{9,10},{10,1... | collective-permute-start | bytes 491528 | tf_op jit(solution)/shard_map/ppermute | solution.py:381
  50.1 1.9 %collective-permute-start.3 = (bf16[5,128,128]{2,1,0:T(8,128)(2,1)S(1)}, bf16[5,128,128]{2,1,0:T(8,128)(2,1)S(1)}, u32[]{:S(2)}, u32[]{:S(2)}) collective-permute-start(bf16[5,128,128]{2,1,0:T(8,128)(2,1)S(1)} %get-tuple-element.35), channel_id=1, source_target_pairs={{1,0},{2,1},{3,2},{4,3},{5,4},{6,5},{7,6},{8,7},{9,8},{10,9},{11,1... | collective-permute-start | bytes 491528 | tf_op jit(solution)/shard_map/ppermute | solution.py:381
  52.1 0.1 collective-permute-start.17
  52.2 0.2 collective-permute-done.2.refs_3_
  52.3 4.4 %collective-permute-done.3.refs_4_ = bf16[5,128,128]{2,1,0:T(8,128)(2,1)S(1)} collective-permute-done((bf16[5,128,128]{2,1,0:T(8,128)(2,1)S(1)}, bf16[5,128,128]{2,1,0:T(8,128)(2,1)S(1)}, u32[]{:S(2)}, u32[]{:S(2)}) %collective-permute-start.3) | collective-permute-done | bytes 163872 | tf_op jit(solution)/shard_map/ppermute | solution.py:381
  56.7 0.6 second_surplus.1
  57.4 4.4 %collective-permute-start.4 = (bf16[64,512]{1,0:T(8,128)(2,1)S(1)}, bf16[64,512]{1,0:T(8,128)(2,1)S(1)}, u32[]{:S(2)}, u32[]{:S(2)}) collective-permute-start(bf16[64,512]{1,0:T(8,128)(2,1)S(1)} %get-tuple-element.40), channel_id=1, source_target_pairs={{0,1},{1,2},{2,3},{3,4},{4,5},{5,6},{6,7},{7,8},{8,9},{9,10},{10,1... | collective-permute-start | bytes 196616 | tf_op jit(solution)/shard_map/ppermute | solution.py:381
  61.8 1.1 %collective-permute-start.6 = (bf16[64,512]{1,0:T(8,128)(2,1)S(1)}, bf16[64,512]{1,0:T(8,128)(2,1)S(1)}, u32[]{:S(2)}, u32[]{:S(2)}) collective-permute-start(bf16[64,512]{1,0:T(8,128)(2,1)S(1)} %get-tuple-element.42), channel_id=1, source_target_pairs={{0,3},{1,4},{2,5},{3,6},{4,7},{5,8},{6,9},{7,10},{8,11},{9,12},{10... | collective-permute-start | bytes 196616 | tf_op jit(solution)/shard_map/ppermute | solution.py:381
  62.9 2.9 %second_own.1 = (bf16[2,64,512]{2,1,0:T(8,128)(2,1)S(1)}, bf16[5,64,512]{2,1,0:T(8,128)(2,1)}) custom-call(s32[5,1,26]{2,1,0:T(1,128)S(1)} %bitcast.15, s32[1,1]{1,0:T(1,128)S(6)} %copy.12.count.refs_1_, bf16[6,128,640]{2,1,0:T(8,128)(2,1)S(1)} %get-tuple-element.33.refs_2_, bf16[5,128,128]{2,1,0:T(8,128)(2,1)S(1)} %collective-permute-done.2.refs_3_, ...), custom_call_target="tpu_custom_call" | custom-call | tf_op jit(solution)/shard_map/second_own/pallas_call | solution.py:537
  65.8 2.0 %collective-permute-done.5.refs_2_ = bf16[64,512]{1,0:T(8,128)(2,1)S(1)} collective-permute-done((bf16[64,512]{1,0:T(8,128)(2,1)S(1)}, bf16[64,512]{1,0:T(8,128)(2,1)S(1)}, u32[]{:S(2)}, u32[]{:S(2)}) %collective-permute-start.5) | collective-permute-done | bytes 65568 | tf_op jit(solution)/shard_map/ppermute | solution.py:381
  67.7 1.2 %collective-permute-done.6.refs_3_ = bf16[64,512]{1,0:T(8,128)(2,1)S(1)} collective-permute-done((bf16[64,512]{1,0:T(8,128)(2,1)S(1)}, bf16[64,512]{1,0:T(8,128)(2,1)S(1)}, u32[]{:S(2)}, u32[]{:S(2)}) %collective-permute-start.6) | collective-permute-done | bytes 65568 | tf_op jit(solution)/shard_map/ppermute | solution.py:381
  68.9 0.7 place.1
  69.6 1.0 %shard_map.115 = (f32[64,1728]{1,0:T(8,128)}, f32[64,1728]{1,0:T(8,128)}) custom-call(bf16[64,1728]{1,0:T(8,128)(2,1)S(1)} %shard_map.114.mine_ref, bf16[64,1728]{1,0:T(8,128)(2,1)S(1)} %collective-permute-done.17.other_ref), custom_call_target="tpu_custom_call" | custom-call | tf_op jit(solution)/shard_map/pallas_call | solution.py:413
  (17 shorter events, 0.1 us)
Async XLA Ops:
  0.6 13.5 %copy-start = (bf16[8,256,256]{2,1,0:T(8,128)(2,1)S(1)}, bf16[8,256,256]{2,1,0:T(8,128)(2,1)}, u32[]{:S(2)}) copy-start(bf16[8,256,256]{2,1,0:T(8,128)(2,1)} %constant.4.clone.move_ref.refs_6_) | copy-start | bytes 3145732
  0.6 1.1 %copy-start.1 = (bf16[1,5,64,512]{3,2,1,0:T(8,128)(2,1)S(1)}, bf16[1,5,64,512]{3,2,1,0:T(8,128)(2,1)}, u32[]{:S(2)}) copy-start(bf16[1,5,64,512]{3,2,1,0:T(8,128)(2,1)} %param.9) | copy-start | bytes 983044
  1.7 1.0 %copy-start.3 = (bf16[1,5,64,512]{3,2,1,0:T(8,128)(2,1)S(1)}, bf16[1,5,64,512]{3,2,1,0:T(8,128)(2,1)}, u32[]{:S(2)}) copy-start(bf16[1,5,64,512]{3,2,1,0:T(8,128)(2,1)} %param.10) | copy-start | bytes 983044
  2.9 10.4 %collective-permute-start = (bf16[5,128,128]{2,1,0:T(8,128)(2,1)S(1)}, bf16[5,128,128]{2,1,0:T(8,128)(2,1)S(1)}, u32[]{:S(2)}, u32[]{:S(2)}) collective-permute-start(bf16[5,128,128]{2,1,0:T(8,128)(2,1)S(1)} %get-tuple-element.29), channel_id=1, source_target_pairs={{0,1},{1,2},{2,3},{3,4},{4,5},{5,6},{6,7},{7,8},{8,9},{9,10},{10,1... | collective-permute-start | bytes 491528 | tf_op jit(solution)/shard_map/ppermute | solution.py:381
  7.4 6.6 %collective-permute-start.1 = (bf16[5,128,128]{2,1,0:T(8,128)(2,1)S(1)}, bf16[5,128,128]{2,1,0:T(8,128)(2,1)S(1)}, u32[]{:S(2)}, u32[]{:S(2)}) collective-permute-start(bf16[5,128,128]{2,1,0:T(8,128)(2,1)S(1)} %get-tuple-element.30), channel_id=1, source_target_pairs={{1,0},{2,1},{3,2},{4,3},{5,4},{6,5},{7,6},{8,7},{9,8},{10,9},{11,1... | collective-permute-start | bytes 491528 | tf_op jit(solution)/shard_map/ppermute | solution.py:381
  10.0 0.9 %copy-start.6 = (bf16[64,1728]{1,0:T(8,128)(2,1)S(1)}, bf16[64,1728]{1,0:T(8,128)(2,1)}, u32[]{:S(2)}) copy-start(bf16[64,1728]{1,0:T(8,128)(2,1)} %one_far.1) | copy-start | bytes 663556
  11.0 0.9 %copy-start.7 = (bf16[64,1728]{1,0:T(8,128)(2,1)S(1)}, bf16[64,1728]{1,0:T(8,128)(2,1)}, u32[]{:S(2)}) copy-start(bf16[64,1728]{1,0:T(8,128)(2,1)} %two_far.1) | copy-start | bytes 663556
  11.9 2.2 %copy-start.5 = (bf16[4,16,640]{2,1,0:T(8,128)(2,1)S(1)}, bf16[4,16,640]{2,1,0:T(8,128)(2,1)}, u32[]{:S(2)}) copy-start(bf16[4,16,640]{2,1,0:T(8,128)(2,1)} %constant.5.clone.edge_ref.refs_5_) | copy-start | bytes 245764
  14.1 0.7 copy-start.8
  17.9 1.9 %collective-permute-start.7 = (f32[64,1728]{1,0:T(8,128)S(1)}, f32[64,1728]{1,0:T(8,128)S(1)}, u32[]{:S(2)}, u32[]{:S(2)}) collective-permute-start(f32[64,1728]{1,0:T(8,128)S(1)} %get-tuple-element.45), channel_id=1, source_target_pairs={{0,1},{1,0},{2,3},{3,2},{4,5},{5,4},{6,7},{7,6},{8,9},{9,8},{10,11... | collective-permute-start | bytes 1327112 | tf_op jit(solution)/shard_map/ppermute | solution.py:409
  19.9 11.3 %collective-permute-start.8 = (bf16[16,1728]{1,0:T(8,128)(2,1)S(1)}, bf16[16,1728]{1,0:T(8,128)(2,1)S(1)}, u32[]{:S(2)}, u32[]{:S(2)}) collective-permute-start(bf16[16,1728]{1,0:T(8,128)(2,1)S(1)} %get-tuple-element.47), channel_id=1, source_target_pairs={{0,2},{1,3},{2,0},{3,1},{4,6},{5,7},{6,4},{7,5},{8,10},{9,11},{10,... | collective-permute-start | bytes 165896 | tf_op jit(solution)/shard_map/ppermute | solution.py:409
  29.3 3.0 %collective-permute-start.9 = (bf16[16,1728]{1,0:T(8,128)(2,1)S(1)}, bf16[16,1728]{1,0:T(8,128)(2,1)S(1)}, u32[]{:S(2)}, u32[]{:S(2)}) collective-permute-start(bf16[16,1728]{1,0:T(8,128)(2,1)S(1)} %get-tuple-element.48), channel_id=1, source_target_pairs={{0,16},{1,17},{2,18},{3,19},{4,20},{5,21},{6,22},{7,23},{8,24},{9,... | collective-permute-start | bytes 165896 | tf_op jit(solution)/shard_map/ppermute | solution.py:409
  29.9 4.0 %collective-permute-start.10 = (bf16[16,1728]{1,0:T(8,128)(2,1)S(1)}, bf16[16,1728]{1,0:T(8,128)(2,1)S(1)}, u32[]{:S(2)}, u32[]{:S(2)}) collective-permute-start(bf16[16,1728]{1,0:T(8,128)(2,1)S(1)} %get-tuple-element.49), channel_id=1, source_target_pairs={{0,18},{1,19},{2,16},{3,17},{4,22},{5,23},{6,20},{7,21},{8,26},{9,... | collective-permute-start | bytes 165896 | tf_op jit(solution)/shard_map/ppermute | solution.py:409
  33.9 22.8 %copy-start.2 = (bf16[1,5,64,512]{3,2,1,0:T(8,128)(2,1)S(1)}, bf16[1,5,64,512]{3,2,1,0:T(8,128)(2,1)}, u32[]{:S(2)}) copy-start(bf16[1,5,64,512]{3,2,1,0:T(8,128)(2,1)} %param.9) | copy-start | bytes 983044
  33.9 22.8 %copy-start.4 = (bf16[1,5,64,512]{3,2,1,0:T(8,128)(2,1)S(1)}, bf16[1,5,64,512]{3,2,1,0:T(8,128)(2,1)}, u32[]{:S(2)}) copy-start(bf16[1,5,64,512]{3,2,1,0:T(8,128)(2,1)} %param.10) | copy-start | bytes 983044
  34.0 4.9 %collective-permute-start.13 = (bf16[16,1728]{1,0:T(8,128)(2,1)S(1)}, bf16[16,1728]{1,0:T(8,128)(2,1)S(1)}, u32[]{:S(2)}, u32[]{:S(2)}) collective-permute-start(bf16[16,1728]{1,0:T(8,128)(2,1)S(1)} %shard_map.112.refs_0_), channel_id=1, source_target_pairs={{0,12},{1,13},{2,14},{3,15},{4,8},{5,9},{6,10},{7,11},{8,4},{9,5},... | collective-permute-start | bytes 165896 | tf_op jit(solution)/shard_map/ppermute | solution.py:409
  35.1 4.5 %collective-permute-start.12 = (bf16[16,1728]{1,0:T(8,128)(2,1)S(1)}, bf16[16,1728]{1,0:T(8,128)(2,1)S(1)}, u32[]{:S(2)}, u32[]{:S(2)}) collective-permute-start(bf16[16,1728]{1,0:T(8,128)(2,1)S(1)} %shard_map.112.refs_0_), channel_id=1, source_target_pairs={{0,8},{1,9},{2,10},{3,11},{4,12},{5,13},{6,14},{7,15},{8,0},{9,1},... | collective-permute-start | bytes 165896 | tf_op jit(solution)/shard_map/ppermute | solution.py:409
  36.5 3.6 %collective-permute-start.11 = (bf16[16,1728]{1,0:T(8,128)(2,1)S(1)}, bf16[16,1728]{1,0:T(8,128)(2,1)S(1)}, u32[]{:S(2)}, u32[]{:S(2)}) collective-permute-start(bf16[16,1728]{1,0:T(8,128)(2,1)S(1)} %shard_map.112.refs_0_), channel_id=1, source_target_pairs={{0,4},{1,5},{2,6},{3,7},{4,0},{5,1},{6,2},{7,3},{8,12},{9,13},{10,... | collective-permute-start | bytes 165896 | tf_op jit(solution)/shard_map/ppermute | solution.py:409
  40.1 11.9 %collective-permute-start.16 = (bf16[16,1728]{1,0:T(8,128)(2,1)S(1)}, bf16[16,1728]{1,0:T(8,128)(2,1)S(1)}, u32[]{:S(2)}, u32[]{:S(2)}) collective-permute-start(bf16[16,1728]{1,0:T(8,128)(2,1)S(1)} %shard_map.113.refs_0_), channel_id=1, source_target_pairs={{0,18},{1,19},{2,16},{3,17},{4,22},{5,23},{6,20},{7,21},{8,26},{9,... | collective-permute-start | bytes 165896 | tf_op jit(solution)/shard_map/ppermute | solution.py:409
  41.3 10.7 %collective-permute-start.15 = (bf16[16,1728]{1,0:T(8,128)(2,1)S(1)}, bf16[16,1728]{1,0:T(8,128)(2,1)S(1)}, u32[]{:S(2)}, u32[]{:S(2)}) collective-permute-start(bf16[16,1728]{1,0:T(8,128)(2,1)S(1)} %shard_map.113.refs_0_), channel_id=1, source_target_pairs={{0,16},{1,17},{2,18},{3,19},{4,20},{5,21},{6,22},{7,23},{8,24},{9,... | collective-permute-start | bytes 165896 | tf_op jit(solution)/shard_map/ppermute | solution.py:409
  42.6 9.4 %collective-permute-start.14 = (bf16[16,1728]{1,0:T(8,128)(2,1)S(1)}, bf16[16,1728]{1,0:T(8,128)(2,1)S(1)}, u32[]{:S(2)}, u32[]{:S(2)}) collective-permute-start(bf16[16,1728]{1,0:T(8,128)(2,1)S(1)} %shard_map.113.refs_0_), channel_id=1, source_target_pairs={{0,2},{1,3},{2,0},{3,1},{4,6},{5,7},{6,4},{7,5},{8,10},{9,11},{10,... | collective-permute-start | bytes 165896 | tf_op jit(solution)/shard_map/ppermute | solution.py:409
  42.8 9.5 %collective-permute-start.2 = (bf16[5,128,128]{2,1,0:T(8,128)(2,1)S(1)}, bf16[5,128,128]{2,1,0:T(8,128)(2,1)S(1)}, u32[]{:S(2)}, u32[]{:S(2)}) collective-permute-start(bf16[5,128,128]{2,1,0:T(8,128)(2,1)S(1)} %get-tuple-element.34), channel_id=1, source_target_pairs={{0,1},{1,2},{2,3},{3,4},{4,5},{5,6},{6,7},{7,8},{8,9},{9,10},{10,1... | collective-permute-start | bytes 491528 | tf_op jit(solution)/shard_map/ppermute | solution.py:381
  50.1 6.6 %collective-permute-start.3 = (bf16[5,128,128]{2,1,0:T(8,128)(2,1)S(1)}, bf16[5,128,128]{2,1,0:T(8,128)(2,1)S(1)}, u32[]{:S(2)}, u32[]{:S(2)}) collective-permute-start(bf16[5,128,128]{2,1,0:T(8,128)(2,1)S(1)} %get-tuple-element.35), channel_id=1, source_target_pairs={{1,0},{2,1},{3,2},{4,3},{5,4},{6,5},{7,6},{8,7},{9,8},{10,9},{11,1... | collective-permute-start | bytes 491528 | tf_op jit(solution)/shard_map/ppermute | solution.py:381
  52.1 17.5 %collective-permute-start.17 = (bf16[64,1728]{1,0:T(8,128)(2,1)S(1)}, bf16[64,1728]{1,0:T(8,128)(2,1)S(1)}, u32[]{:S(2)}, u32[]{:S(2)}) collective-permute-start(bf16[64,1728]{1,0:T(8,128)(2,1)S(1)} %shard_map.114.mine_ref), channel_id=1, source_target_pairs={{0,1},{1,0},{2,3},{3,2},{4,5},{5,4},{6,7},{7,6},{8,9},{9,8},{10,11... | collective-permute-start | bytes 663560 | tf_op jit(solution)/shard_map/ppermute | solution.py:409
  57.4 8.4 %collective-permute-start.4 = (bf16[64,512]{1,0:T(8,128)(2,1)S(1)}, bf16[64,512]{1,0:T(8,128)(2,1)S(1)}, u32[]{:S(2)}, u32[]{:S(2)}) collective-permute-start(bf16[64,512]{1,0:T(8,128)(2,1)S(1)} %get-tuple-element.40), channel_id=1, source_target_pairs={{0,1},{1,2},{2,3},{3,4},{4,5},{5,6},{6,7},{7,8},{8,9},{9,10},{10,1... | collective-permute-start | bytes 196616 | tf_op jit(solution)/shard_map/ppermute | solution.py:381
  61.8 5.9 %collective-permute-start.5 = (bf16[64,512]{1,0:T(8,128)(2,1)S(1)}, bf16[64,512]{1,0:T(8,128)(2,1)S(1)}, u32[]{:S(2)}, u32[]{:S(2)}) collective-permute-start(bf16[64,512]{1,0:T(8,128)(2,1)S(1)} %get-tuple-element.41), channel_id=1, source_target_pairs={{0,2},{1,3},{2,4},{3,5},{4,6},{5,7},{6,8},{7,9},{8,10},{9,11},{10,... | collective-permute-start | bytes 196616 | tf_op jit(solution)/shard_map/ppermute | solution.py:381
  61.8 7.1 %collective-permute-start.6 = (bf16[64,512]{1,0:T(8,128)(2,1)S(1)}, bf16[64,512]{1,0:T(8,128)(2,1)S(1)}, u32[]{:S(2)}, u32[]{:S(2)}) collective-permute-start(bf16[64,512]{1,0:T(8,128)(2,1)S(1)} %get-tuple-element.42), channel_id=1, source_target_pairs={{0,3},{1,4},{2,5},{3,6},{4,7},{5,8},{6,9},{7,10},{8,11},{9,12},{10... | collective-permute-start | bytes 196616 | tf_op jit(solution)/shard_map/ppermute | solution.py:381

commit v3 on v2

--- a/solution.py
+++ b/solution.py
@@ -21,14 +21,7 @@
 TURNS = [(q, r) for q, r in RING if (q, r) != (0, 0)]
 
 
-def turn_tables():
-    cell = np.arange(PLANE)
-    row, column = cell // EDGE, cell % EDGE
-    moves = np.zeros((len(TURNS), 4 * PLANE, 4 * PLANE), np.float32)
-    for number, (q, r) in enumerate(TURNS):
-        source = ((row + q) % EDGE) * EDGE + (column + r) % EDGE
-        for block in range(4):
-            moves[number, block * PLANE + source, block * PLANE + cell] = 1
+def edge_table():
     lane = np.arange(LONG) % PLANE
     edges = np.stack(
         [
@@ -38,8 +31,7 @@
             lane % EDGE == 0,
         ]
     ).astype(np.float32)
-    edges = np.broadcast_to(edges[:, None, :], (4, 16, LONG))
-    return jnp.asarray(moves, jnp.bfloat16), jnp.asarray(edges, jnp.bfloat16)
+    return jnp.asarray(np.broadcast_to(edges[:, None, :], (4, 16, LONG)), jnp.bfloat16)
 
 
 def shifted_right(values):
@@ -63,17 +55,17 @@
         copy.wait()
     front = lax.broadcasted_iota(jnp.int32, (channels, LANES), 1) < PLANE
     for slot in range(slots):
-        for half in range(2):
-            band = slice(half * channels, (half + 1) * channels)
-            late = pltpu.roll(end[half, slot].astype(jnp.float32), PLANE, 1)
-            last_ref[slot, band, :] = jnp.where(front, late, 0.0).astype(jnp.bfloat16)
-            early = pltpu.roll(begin[half, slot].astype(jnp.float32), PLANE, 1)
-            first_ref[slot, band, :] = jnp.where(front, 0.0, early).astype(jnp.bfloat16)
+        late, late_dy = (end[half, slot].astype(jnp.float32) for half in range(2))
+        late = jnp.where(front, pltpu.roll(late, PLANE, 1), late_dy)
+        last_ref[slot] = late.astype(jnp.bfloat16)
+        early, early_dy = (begin[half, slot].astype(jnp.float32) for half in range(2))
+        early = jnp.where(front, early_dy, pltpu.roll(early, PLANE, 1))
+        first_ref[slot] = early.astype(jnp.bfloat16)
 
 
 def prepare(
-    x_far, dy_far, one_far, two_far,
-    long_ref, one_straight, two_straight, one_turned, two_turned,
+    link, x_far, dy_far, one_far, two_far,
+    link_ref, long_ref, one_straight, two_straight, one_turned, two_turned, move_ref,
     x_ref, dy_ref, one_ref, two_ref, sems,
 ):
     pairs = ((x_far, x_ref), (dy_far, dy_ref), (one_far, one_ref), (two_far, two_ref))
@@ -82,6 +74,18 @@
     ]
     for copy in copies:
         copy.start()
+    for slot in range(link.shape[0]):
+        for number in range(link.shape[2]):
+            link_ref[slot, 0, number] = link[slot, 0, number]
+    size = move_ref.shape[1]
+    lane = lax.broadcasted_iota(jnp.int32, (EDGE, size), 1)
+    origin = lax.broadcasted_iota(jnp.int32, (size, size), 0)
+    for number, (q, r) in enumerate(TURNS):
+        row = (lane // EDGE + q) & (EDGE - 1)
+        column = (lane + r) & (EDGE - 1)
+        source = (lane & -PLANE) + row * EDGE + column
+        source = jnp.broadcast_to(source[:1], (size, size))
+        move_ref[number] = jnp.where(origin == source, 1.0, 0.0).astype(jnp.bfloat16)
     for copy in copies:
         copy.wait()
     slots, channels = x_ref.shape[0], x_ref.shape[1]
@@ -124,9 +128,17 @@
 
 
 def gather_sides(slots, low_ref, high_ref, low, high):
+    channels = low_ref.shape[1]
+    front = lax.broadcasted_iota(jnp.int32, (channels, LANES), 1) < PLANE
     for slot in range(slots):
-        low[slot] = low_ref[slot]
-        high[slot] = high_ref[slot]
+        for half in range(2):
+            band = slice(half * channels, (half + 1) * channels)
+            below = low_ref[slot].astype(jnp.float32)
+            above = high_ref[slot].astype(jnp.float32)
+            if half:
+                below, above = pltpu.roll(below, PLANE, 1), pltpu.roll(above, PLANE, 1)
+            low[slot, band, :] = jnp.where(front, below, 0.0).astype(jnp.bfloat16)
+            high[slot, band, :] = jnp.where(front, 0.0, above).astype(jnp.bfloat16)
     low[slots] = jnp.zeros(low.shape[1:], jnp.bfloat16)
     high[slots] = jnp.zeros(high.shape[1:], jnp.bfloat16)
 
@@ -250,8 +262,10 @@
 
     lax.fori_loop(0, count[0, 0], visit, 0)
     for slot in range(slots):
-        last_ref[slot] = inner_ref[slot, :, LONG - LANES :]
-        first_ref[slot] = inner_ref[slot, :, :LANES]
+        for ref, start in ((last_ref, LONG - LANES), (first_ref, 0)):
+            plane = inner_ref[slot, :, start : start + LANES].astype(jnp.float32)
+            plane = plane[:channels] + pltpu.roll(plane[channels:], PLANE, 1)
+            ref[slot] = plane.astype(jnp.bfloat16)
     halves = [keep_ref, give_ref]
     upper = spot(levels[:1]) == 1
 
@@ -452,8 +466,8 @@
     bf16, f32 = jnp.bfloat16, jnp.float32
     shape = jax.ShapeDtypeStruct
     long_shape = shape((slots + 1, 2 * channels, LONG), bf16)
-    side_shape = shape((slots, 2 * channels, LANES), bf16)
-    moves, edges = turn_tables()
+    side_shape = shape((slots, channels, LANES), bf16)
+    edges = edge_table()
     params = pltpu.CompilerParams(vmem_limit_bytes=20 * 2**20)
 
     far = pl.BlockSpec(memory_space=pltpu.HBM)
@@ -471,11 +485,13 @@
         name="sides",
     )(x, dy)
     weight_shape = shape((3 * channels, 9 * channels), bf16)
-    long_in, one_straight, two_straight, one_turned, two_turned = pl.pallas_call(
+    link, long_in, one_straight, two_straight, one_turned, two_turned, moves = pl.pallas_call(
         prepare,
-        out_shape=(long_shape,) + (weight_shape,) * 4,
-        in_specs=[far] * 4,
-        out_specs=tuple(vmem(5)),
+        out_shape=(shape(link.shape, link.dtype), long_shape)
+        + (weight_shape,) * 4
+        + (shape((len(TURNS), 4 * PLANE, 4 * PLANE), bf16),),
+        in_specs=smem(1) + [far] * 4,
+        out_specs=tuple(smem(1) + vmem(6)),
         scratch_shapes=[
             pltpu.VMEM(x.shape, bf16),
             pltpu.VMEM(x.shape, bf16),
@@ -485,7 +501,7 @@
         ],
         compiler_params=params,
         name="prepare",
-    )(x, dy, kernel_one, kernel_two)
+    )(link, x, dy, kernel_one, kernel_two)
     low = step_to(last, 1, False)
     high = step_to(first, -1, False)
     side_scratch = pltpu.VMEM((slots + 1, 2 * channels, LANES), bf16)

time: 70.9 us -> 72.1 us (1.017)
  local copies, waits for them, and re-layouts: 4.6 us -> 2.9 us
  Pallas kernels: 10.2 us -> 11.2 us
    ppermute x11, starting transfers between devices: 17.6 us -> 22.9 us  [swap(): return lax.ppermute(value, ('batch', 'space'), pairs)]
    ppermute x7, starting transfers between devices: 21.1 us -> 16.4 us  [step_to(): return lax.ppermute(x, 'space', pairs)]
    ppermute x11, waiting for transfers between devices: 7.24 us -> 9.77 us  [swap(): return lax.ppermute(value, ('batch', 'space'), pairs)]
    ppermute x7, waiting for transfers between devices: 8.42 us -> 6.53 us  [step_to(): return lax.ppermute(x, 'space', pairs)]
    unnamed x18 -> x16, local copies, waits for them, and re-layouts: 4.6 us -> 2.9 us
    pallas_call x1, Pallas kernels: 1.41 us -> 2.25 us  [shards(): pl.pallas_call(prepare, out_shape=(shape(link.shape, link.dtype), long_sh...]
  transfers between devices with their start and end apart: 18 -> 18, of which waited for: 12 -> 13; matrix products, arithmetic and copies ran while one was open for 0% -> 0% of each run, Pallas kernels for 8% -> 9%
where the time goes in v3:
time: 72.1 us; the launch traced here: 71.3 us
  starting transfers between devices  39.4 us (55%)
  waiting for transfers between devices  16.3 us (23%)
  Pallas kernels  11.2 us (16%)
  local copies, waits for them, and re-layouts  2.9 us (4%)
  between operations  1.47 us (2%)
    ppermute x11, starting transfers between devices, swap(): return lax.ppermute(value, ('batch', 'space'), pairs)  22.9 us
    ppermute x7, starting transfers between devices, step_to(): return lax.ppermute(x, 'space', pairs)  16.4 us
    ppermute x11, waiting for transfers between devices, swap(): return lax.ppermute(value, ('batch', 'space'), pairs)  9.77 us
    ppermute x7, waiting for transfers between devices, step_to(): return lax.ppermute(x, 'space', pairs)  6.53 us
    pallas_call x1, Pallas kernels, shards(): pl.pallas_call(partial(first_half, levels=groups[0]), out_shape=(long_sha...  3.27 us
    pallas_call x1, Pallas kernels, shards(): pl.pallas_call(second_own, out_shape=(shape((WORK_CAP,) + x.shape[1:], bf...  2.94 us
    unnamed x16, local copies, waits for them, and re-layouts  2.9 us
    pallas_call x1, Pallas kernels, shards(): pl.pallas_call(prepare, out_shape=(shape(link.shape, link.dtype), long_sh...  2.25 us
  transfers between devices with their start and end apart: 18, of which 13 were waited for; matrix products, arithmetic and copies ran while one was open for 0% of the time, Pallas kernels for 9%

profile of v3, /device:TPU:1, one launch (start us, length us, event | category | flops | bytes accessed | tf_op | source)
XLA Modules:
  0.0 71.3 jit_solution(3611507291240876531)
XLA Ops:
  0.6 1.0 %copy-done = bf16[1,5,64,512]{3,2,1,0:T(8,128)(2,1)S(1)} copy-done((bf16[1,5,64,512]{3,2,1,0:T(8,128)(2,1)S(1)}, bf16[1,5,64,512]{3,2,1,0:T(8,128)(2,1)}, u32[]{:S(2)}) %copy-start) | copy-done | bytes 327704
  1.6 1.0 %copy-done.2 = bf16[1,5,64,512]{3,2,1,0:T(8,128)(2,1)S(1)} copy-done((bf16[1,5,64,512]{3,2,1,0:T(8,128)(2,1)S(1)}, bf16[1,5,64,512]{3,2,1,0:T(8,128)(2,1)}, u32[]{:S(2)}) %copy-start.2) | copy-done | bytes 327704
  2.6 0.2 sides.1
  2.8 0.0 copy-start.7
  2.8 4.5 %collective-permute-start = (bf16[5,64,128]{2,1,0:T(8,128)(2,1)S(1)}, bf16[5,64,128]{2,1,0:T(8,128)(2,1)S(1)}, u32[]{:S(2)}, u32[]{:S(2)}) collective-permute-start(bf16[5,64,128]{2,1,0:T(8,128)(2,1)S(1)} %get-tuple-element.32), channel_id=1, source_target_pairs={{0,1},{1,2},{2,3},{3,4},{4,5},{5,6},{6,7},{7,8},{8,9},{9,10},{10,1... | collective-permute-start | bytes 245768 | tf_op jit(solution)/shard_map/ppermute | solution.py:395
  7.3 1.9 %collective-permute-start.1 = (bf16[5,64,128]{2,1,0:T(8,128)(2,1)S(1)}, bf16[5,64,128]{2,1,0:T(8,128)(2,1)S(1)}, u32[]{:S(2)}, u32[]{:S(2)}) collective-permute-start(bf16[5,64,128]{2,1,0:T(8,128)(2,1)S(1)} %get-tuple-element.33), channel_id=1, source_target_pairs={{1,0},{2,1},{3,2},{4,3},{5,4},{6,5},{7,6},{8,7},{9,8},{10,9},{11,1... | collective-permute-start | bytes 245768 | tf_op jit(solution)/shard_map/ppermute | solution.py:395
  9.9 0.0 copy-start.6
  9.9 0.9 %copy-done.6 = bf16[64,1728]{1,0:T(8,128)(2,1)S(1)} copy-done((bf16[64,1728]{1,0:T(8,128)(2,1)S(1)}, bf16[64,1728]{1,0:T(8,128)(2,1)}, u32[]{:S(2)}) %copy-start.6) | copy-done | bytes 221208
  10.9 2.2 %prepare.1 = (s32[5,1,26]{2,1,0:T(1,128)S(1)}, bf16[6,128,640]{2,1,0:T(8,128)(2,1)S(1)}, bf16[192,576]{1,0:T(8,128)(2,1)S(1)}, bf16[192,576]{1,0:T(8,128)(2,1)S(...) custom-call(s32[5,1,26]{2,1,0:T(1,128)S(1)} %bitcast.13, ...), custom_call_target="tpu_custom_call" | custom-call | tf_op jit(solution)/shard_map/prepare/pallas_call | solution.py:488
  13.1 0.0 collective-permute-done.low_ref
  13.1 0.0 collective-permute-done.1.high_ref
  13.2 3.3 %first_half.1 = (bf16[6,128,640]{2,1,0:T(8,128)(2,1)S(1)}, bf16[5,64,128]{2,1,0:T(8,128)(2,1)S(1)}, bf16[5,64,128]{2,1,0:T(8,128)(2,1)S(1)}, f32[64,1728]{1,0:T(8,128)S(1)}, f32[64,1728]{1,0:T(8,128)S(1)}) custom-call(s32[5,1,26]{2,1,0:T(1,128)S(1)} %get-tuple-element.30.link.refs_0_, s32[1,1]{1,0:T(1,128)S(6)} %copy.11.count.refs_1_, ...), custom_call_target="tpu_custom_call" | custom-call | tf_op jit(solution)/shard_map/first_half/pallas_call | solution.py:512
  16.4 0.1 collective-permute-start.7
  16.5 1.8 %collective-permute-done.7.got_ref = f32[64,1728]{1,0:T(8,128)S(1)} collective-permute-done((f32[64,1728]{1,0:T(8,128)S(1)}, f32[64,1728]{1,0:T(8,128)S(1)}, u32[]{:S(2)}, u32[]{:S(2)}) %collective-permute-start.7) | collective-permute-done | bytes 442400 | tf_op jit(solution)/shard_map/ppermute | solution.py:423
  18.3 0.1 shard_map.102
  18.4 10.2 %collective-permute-start.8 = (bf16[16,1728]{1,0:T(8,128)(2,1)S(1)}, bf16[16,1728]{1,0:T(8,128)(2,1)S(1)}, u32[]{:S(2)}, u32[]{:S(2)}) collective-permute-start(bf16[16,1728]{1,0:T(8,128)(2,1)S(1)} %get-tuple-element.51), channel_id=1, source_target_pairs={{0,2},{1,3},{2,0},{3,1},{4,6},{5,7},{6,4},{7,5},{8,10},{9,11},{10,... | collective-permute-start | bytes 165896 | tf_op jit(solution)/shard_map/ppermute | solution.py:423
  28.6 1.3 %collective-permute-start.10 = (bf16[16,1728]{1,0:T(8,128)(2,1)S(1)}, bf16[16,1728]{1,0:T(8,128)(2,1)S(1)}, u32[]{:S(2)}, u32[]{:S(2)}) collective-permute-start(bf16[16,1728]{1,0:T(8,128)(2,1)S(1)} %get-tuple-element.53), channel_id=1, source_target_pairs={{0,18},{1,19},{2,16},{3,17},{4,22},{5,23},{6,20},{7,21},{8,26},{9,... | collective-permute-start | bytes 165896 | tf_op jit(solution)/shard_map/ppermute | solution.py:423
  29.8 0.7 collective-permute-done.8.refs_1_
  30.5 1.1 %collective-permute-done.9.refs_2_ = bf16[16,1728]{1,0:T(8,128)(2,1)S(1)} collective-permute-done((bf16[16,1728]{1,0:T(8,128)(2,1)S(1)}, bf16[16,1728]{1,0:T(8,128)(2,1)S(1)}, u32[]{:S(2)}, u32[]{:S(2)}) %collective-permute-start.9) | collective-permute-done | bytes 55328 | tf_op jit(solution)/shard_map/ppermute | solution.py:423
  31.6 0.9 %collective-permute-done.10.refs_3_ = bf16[16,1728]{1,0:T(8,128)(2,1)S(1)} collective-permute-done((bf16[16,1728]{1,0:T(8,128)(2,1)S(1)}, bf16[16,1728]{1,0:T(8,128)(2,1)S(1)}, u32[]{:S(2)}, u32[]{:S(2)}) %collective-permute-start.10) | collective-permute-done | bytes 55328 | tf_op jit(solution)/shard_map/ppermute | solution.py:423
  32.6 0.0 copy-start.3
  32.6 1.0 %collective-permute-start.13 = (bf16[16,1728]{1,0:T(8,128)(2,1)S(1)}, bf16[16,1728]{1,0:T(8,128)(2,1)S(1)}, u32[]{:S(2)}, u32[]{:S(2)}) collective-permute-start(bf16[16,1728]{1,0:T(8,128)(2,1)S(1)} %shard_map.103.refs_0_), channel_id=1, source_target_pairs={{0,12},{1,13},{2,14},{3,15},{4,8},{5,9},{6,10},{7,11},{8,4},{9,5},... | collective-permute-start | bytes 165896 | tf_op jit(solution)/shard_map/ppermute | solution.py:423
  33.6 1.5 %collective-permute-start.12 = (bf16[16,1728]{1,0:T(8,128)(2,1)S(1)}, bf16[16,1728]{1,0:T(8,128)(2,1)S(1)}, u32[]{:S(2)}, u32[]{:S(2)}) collective-permute-start(bf16[16,1728]{1,0:T(8,128)(2,1)S(1)} %shard_map.103.refs_0_), channel_id=1, source_target_pairs={{0,8},{1,9},{2,10},{3,11},{4,12},{5,13},{6,14},{7,15},{8,0},{9,1},... | collective-permute-start | bytes 165896 | tf_op jit(solution)/shard_map/ppermute | solution.py:423
  35.1 1.1 %collective-permute-start.11 = (bf16[16,1728]{1,0:T(8,128)(2,1)S(1)}, bf16[16,1728]{1,0:T(8,128)(2,1)S(1)}, u32[]{:S(2)}, u32[]{:S(2)}) collective-permute-start(bf16[16,1728]{1,0:T(8,128)(2,1)S(1)} %shard_map.103.refs_0_), channel_id=1, source_target_pairs={{0,4},{1,5},{2,6},{3,7},{4,0},{5,1},{6,2},{7,3},{8,12},{9,13},{10,... | collective-permute-start | bytes 165896 | tf_op jit(solution)/shard_map/ppermute | solution.py:423
  36.2 1.3 %collective-permute-done.13.refs_3_ = bf16[16,1728]{1,0:T(8,128)(2,1)S(1)} collective-permute-done((bf16[16,1728]{1,0:T(8,128)(2,1)S(1)}, bf16[16,1728]{1,0:T(8,128)(2,1)S(1)}, u32[]{:S(2)}, u32[]{:S(2)}) %collective-permute-start.13) | collective-permute-done | bytes 55328 | tf_op jit(solution)/shard_map/ppermute | solution.py:423
  37.5 0.6 collective-permute-done.12.refs_2_
  38.1 0.6 collective-permute-done.11.refs_1_
  38.7 1.4 %collective-permute-start.16 = (bf16[16,1728]{1,0:T(8,128)(2,1)S(1)}, bf16[16,1728]{1,0:T(8,128)(2,1)S(1)}, u32[]{:S(2)}, u32[]{:S(2)}) collective-permute-start(bf16[16,1728]{1,0:T(8,128)(2,1)S(1)} %shard_map.104.refs_0_), channel_id=1, source_target_pairs={{0,18},{1,19},{2,16},{3,17},{4,22},{5,23},{6,20},{7,21},{8,26},{9,... | collective-permute-start | bytes 165896 | tf_op jit(solution)/shard_map/ppermute | solution.py:423
  40.1 1.0 %collective-permute-start.15 = (bf16[16,1728]{1,0:T(8,128)(2,1)S(1)}, bf16[16,1728]{1,0:T(8,128)(2,1)S(1)}, u32[]{:S(2)}, u32[]{:S(2)}) collective-permute-start(bf16[16,1728]{1,0:T(8,128)(2,1)S(1)} %shard_map.104.refs_0_), channel_id=1, source_target_pairs={{0,16},{1,17},{2,18},{3,19},{4,20},{5,21},{6,22},{7,23},{8,24},{9,... | collective-permute-start | bytes 165896 | tf_op jit(solution)/shard_map/ppermute | solution.py:423
  41.2 0.3 collective-permute-start.14
  41.4 1.3 %collective-permute-done.16.refs_3_ = bf16[16,1728]{1,0:T(8,128)(2,1)S(1)} collective-permute-done((bf16[16,1728]{1,0:T(8,128)(2,1)S(1)}, bf16[16,1728]{1,0:T(8,128)(2,1)S(1)}, u32[]{:S(2)}, u32[]{:S(2)}) %collective-permute-start.16) | collective-permute-done | bytes 55328 | tf_op jit(solution)/shard_map/ppermute | solution.py:423
  42.7 0.6 collective-permute-done.15.refs_2_
  43.3 0.9 %collective-permute-done.14.refs_1_ = bf16[16,1728]{1,0:T(8,128)(2,1)S(1)} collective-permute-done((bf16[16,1728]{1,0:T(8,128)(2,1)S(1)}, bf16[16,1728]{1,0:T(8,128)(2,1)S(1)}, u32[]{:S(2)}, u32[]{:S(2)}) %collective-permute-start.14) | collective-permute-done | bytes 55328 | tf_op jit(solution)/shard_map/ppermute | solution.py:423
  44.2 5.1 %collective-permute-start.17 = (bf16[64,1728]{1,0:T(8,128)(2,1)S(1)}, bf16[64,1728]{1,0:T(8,128)(2,1)S(1)}, u32[]{:S(2)}, u32[]{:S(2)}) collective-permute-start(bf16[64,1728]{1,0:T(8,128)(2,1)S(1)} %shard_map.105.mine_ref), channel_id=1, source_target_pairs={{0,1},{1,0},{2,3},{3,2},{4,5},{5,4},{6,7},{7,6},{8,9},{9,8},{10,11... | collective-permute-start | bytes 663560 | tf_op jit(solution)/shard_map/ppermute | solution.py:423
  49.4 2.1 %collective-permute-start.2 = (bf16[5,64,128]{2,1,0:T(8,128)(2,1)S(1)}, bf16[5,64,128]{2,1,0:T(8,128)(2,1)S(1)}, u32[]{:S(2)}, u32[]{:S(2)}) collective-permute-start(bf16[5,64,128]{2,1,0:T(8,128)(2,1)S(1)} %get-tuple-element.38), channel_id=1, source_target_pairs={{0,1},{1,2},{2,3},{3,4},{4,5},{5,6},{6,7},{7,8},{8,9},{9,10},{10,1... | collective-permute-start | bytes 245768 | tf_op jit(solution)/shard_map/ppermute | solution.py:395
  51.4 2.2 %collective-permute-start.3 = (bf16[5,64,128]{2,1,0:T(8,128)(2,1)S(1)}, bf16[5,64,128]{2,1,0:T(8,128)(2,1)S(1)}, u32[]{:S(2)}, u32[]{:S(2)}) collective-permute-start(bf16[5,64,128]{2,1,0:T(8,128)(2,1)S(1)} %get-tuple-element.39), channel_id=1, source_target_pairs={{1,0},{2,1},{3,2},{4,3},{5,4},{6,5},{7,6},{8,7},{9,8},{10,9},{11,1... | collective-permute-start | bytes 245768 | tf_op jit(solution)/shard_map/ppermute | solution.py:395
  53.7 0.0 collective-permute-done.2.refs_3_
  53.7 3.5 %collective-permute-done.3.refs_4_ = bf16[5,64,128]{2,1,0:T(8,128)(2,1)S(1)} collective-permute-done((bf16[5,64,128]{2,1,0:T(8,128)(2,1)S(1)}, bf16[5,64,128]{2,1,0:T(8,128)(2,1)S(1)}, u32[]{:S(2)}, u32[]{:S(2)}) %collective-permute-start.3) | collective-permute-done | bytes 81952 | tf_op jit(solution)/shard_map/ppermute | solution.py:395
  57.2 0.7 second_surplus.1
  57.9 4.6 %collective-permute-start.4 = (bf16[64,512]{1,0:T(8,128)(2,1)S(1)}, bf16[64,512]{1,0:T(8,128)(2,1)S(1)}, u32[]{:S(2)}, u32[]{:S(2)}) collective-permute-start(bf16[64,512]{1,0:T(8,128)(2,1)S(1)} %get-tuple-element.44), channel_id=1, source_target_pairs={{0,1},{1,2},{2,3},{3,4},{4,5},{5,6},{6,7},{7,8},{8,9},{9,10},{10,1... | collective-permute-start | bytes 196616 | tf_op jit(solution)/shard_map/ppermute | solution.py:395
  62.5 1.1 %collective-permute-start.6 = (bf16[64,512]{1,0:T(8,128)(2,1)S(1)}, bf16[64,512]{1,0:T(8,128)(2,1)S(1)}, u32[]{:S(2)}, u32[]{:S(2)}) collective-permute-start(bf16[64,512]{1,0:T(8,128)(2,1)S(1)} %get-tuple-element.46), channel_id=1, source_target_pairs={{0,3},{1,4},{2,5},{3,6},{4,7},{5,8},{6,9},{7,10},{8,11},{9,12},{10... | collective-permute-start | bytes 196616 | tf_op jit(solution)/shard_map/ppermute | solution.py:395
  63.6 2.9 %second_own.1 = (bf16[2,64,512]{2,1,0:T(8,128)(2,1)S(1)}, bf16[5,64,512]{2,1,0:T(8,128)(2,1)}) custom-call(s32[5,1,26]{2,1,0:T(1,128)S(1)} %get-tuple-element.30.link.refs_0_, s32[1,1]{1,0:T(1,128)S(6)} %copy.11.count.refs_1_, bf16[6,128,640]{2,1,0:T(8,128)(2,1)S(1)} %get-tuple-element.37.refs_2_, bf16[5,64,128]{2,1,0:T(8,128)(2,1)S(1)} %collective-permute-done.2.refs_3_, ...), custom_call_target="tpu_custom_call" | custom-call | tf_op jit(solution)/shard_map/second_own/pallas_call | solution.py:553
  66.5 0.0 collective-permute-done.4.refs_1_
  66.6 1.9 %collective-permute-done.5.refs_2_ = bf16[64,512]{1,0:T(8,128)(2,1)S(1)} collective-permute-done((bf16[64,512]{1,0:T(8,128)(2,1)S(1)}, bf16[64,512]{1,0:T(8,128)(2,1)S(1)}, u32[]{:S(2)}, u32[]{:S(2)}) %collective-permute-start.5) | collective-permute-done | bytes 65568 | tf_op jit(solution)/shard_map/ppermute | solution.py:395
  68.4 1.2 %collective-permute-done.6.refs_3_ = bf16[64,512]{1,0:T(8,128)(2,1)S(1)} collective-permute-done((bf16[64,512]{1,0:T(8,128)(2,1)S(1)}, bf16[64,512]{1,0:T(8,128)(2,1)S(1)}, u32[]{:S(2)}, u32[]{:S(2)}) %collective-permute-start.6) | collective-permute-done | bytes 65568 | tf_op jit(solution)/shard_map/ppermute | solution.py:395
  69.6 0.7 place.1
  70.2 0.0 collective-permute-done.17.other_ref
  70.2 1.0 %shard_map.106 = (f32[64,1728]{1,0:T(8,128)}, f32[64,1728]{1,0:T(8,128)}) custom-call(bf16[64,1728]{1,0:T(8,128)(2,1)S(1)} %shard_map.105.mine_ref, bf16[64,1728]{1,0:T(8,128)(2,1)S(1)} %collective-permute-done.17.other_ref), custom_call_target="tpu_custom_call" | custom-call | tf_op jit(solution)/shard_map/pallas_call | solution.py:427
  (15 shorter events, 0.1 us)
Async XLA Ops:
  0.6 1.0 %copy-start = (bf16[1,5,64,512]{3,2,1,0:T(8,128)(2,1)S(1)}, bf16[1,5,64,512]{3,2,1,0:T(8,128)(2,1)}, u32[]{:S(2)}) copy-start(bf16[1,5,64,512]{3,2,1,0:T(8,128)(2,1)} %param.8) | copy-start | bytes 983044
  1.6 1.0 %copy-start.2 = (bf16[1,5,64,512]{3,2,1,0:T(8,128)(2,1)S(1)}, bf16[1,5,64,512]{3,2,1,0:T(8,128)(2,1)}, u32[]{:S(2)}) copy-start(bf16[1,5,64,512]{3,2,1,0:T(8,128)(2,1)} %param.9) | copy-start | bytes 983044
  2.6 7.3 %copy-start.1 = (bf16[1,5,64,512]{3,2,1,0:T(8,128)(2,1)S(1)}, bf16[1,5,64,512]{3,2,1,0:T(8,128)(2,1)}, u32[]{:S(2)}) copy-start(bf16[1,5,64,512]{3,2,1,0:T(8,128)(2,1)} %param.8) | copy-start | bytes 983044
  2.6 7.3 %copy-start.5 = (bf16[64,1728]{1,0:T(8,128)(2,1)S(1)}, bf16[64,1728]{1,0:T(8,128)(2,1)}, u32[]{:S(2)}) copy-start(bf16[64,1728]{1,0:T(8,128)(2,1)} %one_far.1) | copy-start | bytes 663556
  2.8 7.1 %copy-start.7 = (s32[1,26,5]{1,0,2:T(1,128)S(1)}, s32[1,26,5]{1,0,2:T(1,128)}, u32[]{:S(2)}) copy-start(s32[1,26,5]{1,0,2:T(1,128)} %param.11) | copy-start | bytes 1564
  2.8 10.3 %collective-permute-start = (bf16[5,64,128]{2,1,0:T(8,128)(2,1)S(1)}, bf16[5,64,128]{2,1,0:T(8,128)(2,1)S(1)}, u32[]{:S(2)}, u32[]{:S(2)}) collective-permute-start(bf16[5,64,128]{2,1,0:T(8,128)(2,1)S(1)} %get-tuple-element.32), channel_id=1, source_target_pairs={{0,1},{1,2},{2,3},{3,4},{4,5},{5,6},{6,7},{7,8},{8,9},{9,10},{10,1... | collective-permute-start | bytes 245768 | tf_op jit(solution)/shard_map/ppermute | solution.py:395
  7.3 5.8 %collective-permute-start.1 = (bf16[5,64,128]{2,1,0:T(8,128)(2,1)S(1)}, bf16[5,64,128]{2,1,0:T(8,128)(2,1)S(1)}, u32[]{:S(2)}, u32[]{:S(2)}) collective-permute-start(bf16[5,64,128]{2,1,0:T(8,128)(2,1)S(1)} %get-tuple-element.33), channel_id=1, source_target_pairs={{1,0},{2,1},{3,2},{4,3},{5,4},{6,5},{7,6},{8,7},{9,8},{10,9},{11,1... | collective-permute-start | bytes 245768 | tf_op jit(solution)/shard_map/ppermute | solution.py:395
  9.9 0.9 %copy-start.6 = (bf16[64,1728]{1,0:T(8,128)(2,1)S(1)}, bf16[64,1728]{1,0:T(8,128)(2,1)}, u32[]{:S(2)}) copy-start(bf16[64,1728]{1,0:T(8,128)(2,1)} %two_far.1) | copy-start | bytes 663556
  10.9 2.3 %copy-start.4 = (bf16[4,16,640]{2,1,0:T(8,128)(2,1)S(1)}, bf16[4,16,640]{2,1,0:T(8,128)(2,1)}, u32[]{:S(2)}) copy-start(bf16[4,16,640]{2,1,0:T(8,128)(2,1)} %constant.2.clone.edge_ref.refs_5_) | copy-start | bytes 245764
  16.4 1.9 %collective-permute-start.7 = (f32[64,1728]{1,0:T(8,128)S(1)}, f32[64,1728]{1,0:T(8,128)S(1)}, u32[]{:S(2)}, u32[]{:S(2)}) collective-permute-start(f32[64,1728]{1,0:T(8,128)S(1)} %get-tuple-element.49), channel_id=1, source_target_pairs={{0,1},{1,0},{2,3},{3,2},{4,5},{5,4},{6,7},{7,6},{8,9},{9,8},{10,11... | collective-permute-start | bytes 1327112 | tf_op jit(solution)/shard_map/ppermute | solution.py:423
  18.4 12.1 %collective-permute-start.8 = (bf16[16,1728]{1,0:T(8,128)(2,1)S(1)}, bf16[16,1728]{1,0:T(8,128)(2,1)S(1)}, u32[]{:S(2)}, u32[]{:S(2)}) collective-permute-start(bf16[16,1728]{1,0:T(8,128)(2,1)S(1)} %get-tuple-element.51), channel_id=1, source_target_pairs={{0,2},{1,3},{2,0},{3,1},{4,6},{5,7},{6,4},{7,5},{8,10},{9,11},{10,... | collective-permute-start | bytes 165896 | tf_op jit(solution)/shard_map/ppermute | solution.py:423
  28.6 3.0 %collective-permute-start.9 = (bf16[16,1728]{1,0:T(8,128)(2,1)S(1)}, bf16[16,1728]{1,0:T(8,128)(2,1)S(1)}, u32[]{:S(2)}, u32[]{:S(2)}) collective-permute-start(bf16[16,1728]{1,0:T(8,128)(2,1)S(1)} %get-tuple-element.52), channel_id=1, source_target_pairs={{0,16},{1,17},{2,18},{3,19},{4,20},{5,21},{6,22},{7,23},{8,24},{9,... | collective-permute-start | bytes 165896 | tf_op jit(solution)/shard_map/ppermute | solution.py:423
  28.6 4.0 %collective-permute-start.10 = (bf16[16,1728]{1,0:T(8,128)(2,1)S(1)}, bf16[16,1728]{1,0:T(8,128)(2,1)S(1)}, u32[]{:S(2)}, u32[]{:S(2)}) collective-permute-start(bf16[16,1728]{1,0:T(8,128)(2,1)S(1)} %get-tuple-element.53), channel_id=1, source_target_pairs={{0,18},{1,19},{2,16},{3,17},{4,22},{5,23},{6,20},{7,21},{8,26},{9,... | collective-permute-start | bytes 165896 | tf_op jit(solution)/shard_map/ppermute | solution.py:423
  32.6 24.6 %copy-start.3 = (bf16[1,5,64,512]{3,2,1,0:T(8,128)(2,1)S(1)}, bf16[1,5,64,512]{3,2,1,0:T(8,128)(2,1)}, u32[]{:S(2)}) copy-start(bf16[1,5,64,512]{3,2,1,0:T(8,128)(2,1)} %param.9) | copy-start | bytes 983044
  32.6 4.9 %collective-permute-start.13 = (bf16[16,1728]{1,0:T(8,128)(2,1)S(1)}, bf16[16,1728]{1,0:T(8,128)(2,1)S(1)}, u32[]{:S(2)}, u32[]{:S(2)}) collective-permute-start(bf16[16,1728]{1,0:T(8,128)(2,1)S(1)} %shard_map.103.refs_0_), channel_id=1, source_target_pairs={{0,12},{1,13},{2,14},{3,15},{4,8},{5,9},{6,10},{7,11},{8,4},{9,5},... | collective-permute-start | bytes 165896 | tf_op jit(solution)/shard_map/ppermute | solution.py:423
  33.6 4.5 %collective-permute-start.12 = (bf16[16,1728]{1,0:T(8,128)(2,1)S(1)}, bf16[16,1728]{1,0:T(8,128)(2,1)S(1)}, u32[]{:S(2)}, u32[]{:S(2)}) collective-permute-start(bf16[16,1728]{1,0:T(8,128)(2,1)S(1)} %shard_map.103.refs_0_), channel_id=1, source_target_pairs={{0,8},{1,9},{2,10},{3,11},{4,12},{5,13},{6,14},{7,15},{8,0},{9,1},... | collective-permute-start | bytes 165896 | tf_op jit(solution)/shard_map/ppermute | solution.py:423
  35.1 3.6 %collective-permute-start.11 = (bf16[16,1728]{1,0:T(8,128)(2,1)S(1)}, bf16[16,1728]{1,0:T(8,128)(2,1)S(1)}, u32[]{:S(2)}, u32[]{:S(2)}) collective-permute-start(bf16[16,1728]{1,0:T(8,128)(2,1)S(1)} %shard_map.103.refs_0_), channel_id=1, source_target_pairs={{0,4},{1,5},{2,6},{3,7},{4,0},{5,1},{6,2},{7,3},{8,12},{9,13},{10,... | collective-permute-start | bytes 165896 | tf_op jit(solution)/shard_map/ppermute | solution.py:423
  38.7 4.0 %collective-permute-start.16 = (bf16[16,1728]{1,0:T(8,128)(2,1)S(1)}, bf16[16,1728]{1,0:T(8,128)(2,1)S(1)}, u32[]{:S(2)}, u32[]{:S(2)}) collective-permute-start(bf16[16,1728]{1,0:T(8,128)(2,1)S(1)} %shard_map.104.refs_0_), channel_id=1, source_target_pairs={{0,18},{1,19},{2,16},{3,17},{4,22},{5,23},{6,20},{7,21},{8,26},{9,... | collective-permute-start | bytes 165896 | tf_op jit(solution)/shard_map/ppermute | solution.py:423
  40.1 3.2 %collective-permute-start.15 = (bf16[16,1728]{1,0:T(8,128)(2,1)S(1)}, bf16[16,1728]{1,0:T(8,128)(2,1)S(1)}, u32[]{:S(2)}, u32[]{:S(2)}) collective-permute-start(bf16[16,1728]{1,0:T(8,128)(2,1)S(1)} %shard_map.104.refs_0_), channel_id=1, source_target_pairs={{0,16},{1,17},{2,18},{3,19},{4,20},{5,21},{6,22},{7,23},{8,24},{9,... | collective-permute-start | bytes 165896 | tf_op jit(solution)/shard_map/ppermute | solution.py:423
  41.2 3.0 %collective-permute-start.14 = (bf16[16,1728]{1,0:T(8,128)(2,1)S(1)}, bf16[16,1728]{1,0:T(8,128)(2,1)S(1)}, u32[]{:S(2)}, u32[]{:S(2)}) collective-permute-start(bf16[16,1728]{1,0:T(8,128)(2,1)S(1)} %shard_map.104.refs_0_), channel_id=1, source_target_pairs={{0,2},{1,3},{2,0},{3,1},{4,6},{5,7},{6,4},{7,5},{8,10},{9,11},{10,... | collective-permute-start | bytes 165896 | tf_op jit(solution)/shard_map/ppermute | solution.py:423
  44.2 26.0 %collective-permute-start.17 = (bf16[64,1728]{1,0:T(8,128)(2,1)S(1)}, bf16[64,1728]{1,0:T(8,128)(2,1)S(1)}, u32[]{:S(2)}, u32[]{:S(2)}) collective-permute-start(bf16[64,1728]{1,0:T(8,128)(2,1)S(1)} %shard_map.105.mine_ref), channel_id=1, source_target_pairs={{0,1},{1,0},{2,3},{3,2},{4,5},{5,4},{6,7},{7,6},{8,9},{9,8},{10,11... | collective-permute-start | bytes 663560 | tf_op jit(solution)/shard_map/ppermute | solution.py:423
  49.4 4.3 %collective-permute-start.2 = (bf16[5,64,128]{2,1,0:T(8,128)(2,1)S(1)}, bf16[5,64,128]{2,1,0:T(8,128)(2,1)S(1)}, u32[]{:S(2)}, u32[]{:S(2)}) collective-permute-start(bf16[5,64,128]{2,1,0:T(8,128)(2,1)S(1)} %get-tuple-element.38), channel_id=1, source_target_pairs={{0,1},{1,2},{2,3},{3,4},{4,5},{5,6},{6,7},{7,8},{8,9},{9,10},{10,1... | collective-permute-start | bytes 245768 | tf_op jit(solution)/shard_map/ppermute | solution.py:395
  51.4 5.8 %collective-permute-start.3 = (bf16[5,64,128]{2,1,0:T(8,128)(2,1)S(1)}, bf16[5,64,128]{2,1,0:T(8,128)(2,1)S(1)}, u32[]{:S(2)}, u32[]{:S(2)}) collective-permute-start(bf16[5,64,128]{2,1,0:T(8,128)(2,1)S(1)} %get-tuple-element.39), channel_id=1, source_target_pairs={{1,0},{2,1},{3,2},{4,3},{5,4},{6,5},{7,6},{8,7},{9,8},{10,9},{11,1... | collective-permute-start | bytes 245768 | tf_op jit(solution)/shard_map/ppermute | solution.py:395
  57.9 8.6 %collective-permute-start.4 = (bf16[64,512]{1,0:T(8,128)(2,1)S(1)}, bf16[64,512]{1,0:T(8,128)(2,1)S(1)}, u32[]{:S(2)}, u32[]{:S(2)}) collective-permute-start(bf16[64,512]{1,0:T(8,128)(2,1)S(1)} %get-tuple-element.44), channel_id=1, source_target_pairs={{0,1},{1,2},{2,3},{3,4},{4,5},{5,6},{6,7},{7,8},{8,9},{9,10},{10,1... | collective-permute-start | bytes 196616 | tf_op jit(solution)/shard_map/ppermute | solution.py:395
  62.5 5.9 %collective-permute-start.5 = (bf16[64,512]{1,0:T(8,128)(2,1)S(1)}, bf16[64,512]{1,0:T(8,128)(2,1)S(1)}, u32[]{:S(2)}, u32[]{:S(2)}) collective-permute-start(bf16[64,512]{1,0:T(8,128)(2,1)S(1)} %get-tuple-element.45), channel_id=1, source_target_pairs={{0,2},{1,3},{2,4},{3,5},{4,6},{5,7},{6,8},{7,9},{8,10},{9,11},{10,... | collective-permute-start | bytes 196616 | tf_op jit(solution)/shard_map/ppermute | solution.py:395
  62.5 7.1 %collective-permute-start.6 = (bf16[64,512]{1,0:T(8,128)(2,1)S(1)}, bf16[64,512]{1,0:T(8,128)(2,1)S(1)}, u32[]{:S(2)}, u32[]{:S(2)}) collective-permute-start(bf16[64,512]{1,0:T(8,128)(2,1)S(1)} %get-tuple-element.46), channel_id=1, source_target_pairs={{0,3},{1,4},{2,5},{3,6},{4,7},{5,8},{6,9},{7,10},{8,11},{9,12},{10... | collective-permute-start | bytes 196616 | tf_op jit(solution)/shard_map/ppermute | solution.py:395
